TPU v7x, 32 devices: a whole 2x2x4 slice. The times are simulated.
32 devices in a mesh: dp: 4 (over y, x), ep: 8 (over z, core).
Axes of the slice: x: 2, y: 2, z: 4, core: 2. Of those that a mesh axis runs over, the one named last changes fastest.
Arguments:
- tokens: bfloat16 [4096, 7168], P(('dp', 'ep')), may hold values from -6 to 6
- out_grad: bfloat16 [4096, 7168], P(('dp', 'ep')), may hold values from -3 to 3
- route_weight: float32 [4096, 1], P(('dp', 'ep')), may hold values from 0.2 to 1
- expert_ids: int32 [4096, 1], P(('dp', 'ep')), may hold values from 0 to 1
- w_gate: bfloat16 [1024, 14336], P('dp', 'ep'), may hold values from -0.0625 to 0.0625
- w_up: bfloat16 [1024, 14336], P('dp', 'ep'), may hold values from -0.0625 to 0.0625
- w_down: bfloat16 [1024, 14336], P('dp', 'ep'), may hold values from -0.1875 to 0.1875
Outputs:
- in_grad: bfloat16 [4096, 7168], P(('dp', 'ep'))
- grad_gate: bfloat16 [1024, 14336], P('dp', 'ep')
- grad_up: bfloat16 [1024, 14336], P('dp', 'ep')
- grad_down: bfloat16 [1024, 14336], P('dp', 'ep')
All inputs are finite; a program needn't handle non-finite values.
Results may differ from a plain program's by a relative error of at most 0.012.
Values may be sent and summed in bfloat16 or wider, within the bound.
A program may use at most 128 MiB of HBM per device.

v0:
```python
import jax
import jax.numpy as jnp
from jax import lax
from jax.sharding import PartitionSpec as P

D = 7168
GROUP = 4
TOP = 1


CONTRACT_LAST = (((1,), (1,)), ((), ()))
CONTRACT_FIRST = (((0,), (0,)), ((), ()))


def as_sent(value):

    def short(part):
        return part.astype(jnp.bfloat16) if part.dtype == jnp.float32 else part

    return jax.tree.map(short, value)


def from_partner(value, axis, distance):
    mask = 2**distance
    pairs = [(source, source ^ mask) for source in range(lax.axis_size(axis))]
    return lax.ppermute(value, axis, pairs)


def slot_tables(expert_ids, route_weight, experts, capacity):
    token_count, top_count = expert_ids.shape
    pair_count = token_count * top_count
    flat_ids = expert_ids.reshape(pair_count)
    onehot = (flat_ids[:, None] == jnp.arange(experts, dtype=jnp.int32)[None, :]).astype(jnp.int32)
    before = jnp.cumsum(onehot, axis=0) - onehot
    ranks = jnp.sum(before * onehot, axis=1)
    kept = ranks < capacity
    slots = jnp.where(kept, flat_ids * capacity + ranks, 0)
    slot_ids = jnp.arange(experts * capacity, dtype=jnp.int32)
    match = (slots[None, :] == slot_ids[:, None]) & kept[None, :]
    pair_ids = jnp.arange(pair_count, dtype=jnp.int32)
    pair_of_slot = jnp.sum(jnp.where(match, pair_ids[None, :], 0), axis=1)
    filled = jnp.any(match, axis=1)
    flat_weight = route_weight.reshape(pair_count)
    weight_of_slot = jnp.sum(jnp.where(match, flat_weight[None, :], jnp.float32(0.0)), axis=1)
    return (kept, slots, pair_of_slot // top_count, filled, weight_of_slot)


def activations(gate, up, back):
    logistic = jax.nn.sigmoid(gate)
    silu = gate * logistic
    hidden = (silu * up).astype(jnp.bfloat16)
    d_gate = (back * up * logistic * (1.0 + gate * (1.0 - logistic))).astype(jnp.bfloat16)
    d_up = (back * silu).astype(jnp.bfloat16)
    return (hidden, d_gate, d_up)


def to_owners(rows, experts, capacity, quarter):
    shaped = rows.reshape(experts, capacity, GROUP, quarter).transpose(0, 2, 1, 3)
    return shaped.reshape(experts * GROUP, capacity, quarter)


def body(tokens, out_grad, route_weight, expert_ids, w_gate, w_up, w_down):
    devices_ep = lax.axis_size("ep")
    experts = devices_ep // GROUP
    token_count = tokens.shape[0]
    capacity = 6 * GROUP * token_count * TOP // (8 * devices_ep)
    quarter = D // GROUP
    levels = GROUP.bit_length() - 1
    kept, slots, token_of_slot, filled, weight_of_slot = slot_tables(
        expert_ids, route_weight, experts, capacity
    )
    x_slots = jnp.take(tokens, token_of_slot, axis=0) * filled[:, None].astype(jnp.bfloat16)
    d_slots = (
        jnp.take(out_grad, token_of_slot, axis=0).astype(jnp.float32) * weight_of_slot[:, None]
    ).astype(jnp.bfloat16)
    x_send = to_owners(x_slots, experts, capacity, quarter)
    d_send = to_owners(d_slots, experts, capacity, quarter)
    x_recv, d_recv = (
        lax.all_to_all(x_send, "ep", split_axis=0, concat_axis=0, tiled=True),
        lax.all_to_all(d_send, "ep", split_axis=0, concat_axis=0, tiled=True),
    )
    row_count = x_recv.shape[0] * x_recv.shape[1]
    x_rows = x_recv.reshape(row_count, quarter)
    d_rows = d_recv.reshape(row_count, quarter)
    gate_w, up_w, down_w = (
        lax.all_gather(w_gate, "dp", axis=0, tiled=True),
        lax.all_gather(w_up, "dp", axis=0, tiled=True),
        lax.all_gather(w_down, "dp", axis=0, tiled=True),
    )
    x_used, d_used = (x_rows, d_rows)
    gate_part = lax.dot_general(
        x_used, gate_w, CONTRACT_LAST, preferred_element_type=jnp.float32
    ).astype(jnp.bfloat16)
    up_part = lax.dot_general(
        x_used, up_w, CONTRACT_LAST, preferred_element_type=jnp.float32
    ).astype(jnp.bfloat16)
    back_part = lax.dot_general(
        d_used, down_w, CONTRACT_LAST, preferred_element_type=jnp.float32
    ).astype(jnp.bfloat16)
    member = lax.axis_index("ep") % GROUP
    pieces = (gate_part[None], up_part[None], back_part[None])
    width = gate_part.shape[1]
    for bit in reversed(range(levels)):
        half = width // 2
        side = member // (1 << bit) % 2
        keep = tuple((lax.dynamic_slice_in_dim(piece, side * half, half, 2) for piece in pieces))
        give = tuple(
            (lax.dynamic_slice_in_dim(piece, (1 - side) * half, half, 2) for piece in pieces)
        )
        received = jax.tree.map(
            lambda part, own: part.astype(own.dtype), from_partner(as_sent(give), "ep", bit), give
        )
        pieces = tuple(
            (jnp.concatenate([mine, theirs], axis=0) for mine, theirs in zip(keep, received))
        )
        width = half
    gate = jnp.sum(pieces[0].astype(jnp.float32), axis=0)
    up = jnp.sum(pieces[1].astype(jnp.float32), axis=0)
    back = jnp.sum(pieces[2].astype(jnp.float32), axis=0)
    shares = activations(gate, up, back)
    for bit in range(levels):
        side = member // (1 << bit) % 2
        other = jax.tree.map(
            lambda part, own: part.astype(own.dtype),
            from_partner(as_sent(shares), "ep", bit),
            shares,
        )
        shares = tuple(
            (
                jnp.where(
                    side == 0,
                    jnp.concatenate([mine, theirs], axis=1),
                    jnp.concatenate([theirs, mine], axis=1),
                )
                for mine, theirs in zip(shares, other)
            )
        )
    hidden, d_gate, d_up = shares
    expert_dx = (
        jnp.dot(d_gate, gate_w, preferred_element_type=jnp.float32)
        + jnp.dot(d_up, up_w, preferred_element_type=jnp.float32)
    ).astype(jnp.bfloat16)
    gate_term = lax.dot_general(d_gate, x_rows, CONTRACT_FIRST, preferred_element_type=jnp.float32)
    up_term = lax.dot_general(d_up, x_rows, CONTRACT_FIRST, preferred_element_type=jnp.float32)
    down_term = lax.dot_general(hidden, d_rows, CONTRACT_FIRST, preferred_element_type=jnp.float32)
    sums = lax.psum_scatter(
        jnp.concatenate([gate_term, up_term, down_term], axis=1).astype(jnp.bfloat16),
        "dp",
        scatter_dimension=0,
        tiled=True,
    ).astype(jnp.float32)
    grad_gate = sums[:, :quarter].astype(jnp.bfloat16)
    grad_up = sums[:, quarter : 2 * quarter].astype(jnp.bfloat16)
    grad_down = sums[:, 2 * quarter :].astype(jnp.bfloat16)
    returned = lax.all_to_all(
        expert_dx.reshape(devices_ep, capacity, quarter),
        "ep",
        split_axis=0,
        concat_axis=0,
        tiled=True,
    )
    slot_rows = (
        returned.reshape(experts, GROUP, capacity, quarter)
        .transpose(0, 2, 1, 3)
        .reshape(experts * capacity, D)
    )
    pair_rows = jnp.take(slot_rows, slots, axis=0) * kept[:, None].astype(jnp.bfloat16)
    in_grad = jnp.sum(pair_rows.reshape(token_count, TOP, D).astype(jnp.float32), axis=1).astype(
        jnp.bfloat16
    )
    return (in_grad, grad_gate, grad_up, grad_down)


def solution(mesh):
    placed = (
        P(("dp", "ep"), None),
        P(("dp", "ep"), None),
        P(("dp", "ep"), None),
        P(("dp", "ep"), None),
        P("dp", "ep"),
        P("dp", "ep"),
        P("dp", "ep"),
    )
    return jax.shard_map(
        body,
        mesh=mesh,
        in_specs=placed,
        out_specs=(P(("dp", "ep"), None), P("dp", "ep"), P("dp", "ep"), P("dp", "ep")),
        check_vma=False,
    )
```

profile of v0, /device:TPU:0, one launch (start us, length us, event | category | flops | bytes accessed | tf_op | source)
XLA Modules:
  0.0 337.3 jit_solution(7923308384006601313)
XLA Ops:
  7.2 0.7 all-gather.8.cloned.1.call-update
  8.0 0.7 all-gather.6.cloned.1.call-update
  8.7 0.7 all-gather.4.cloned.1.call-update
  9.5 0.2 reduce_window_sum.11
  9.7 0.2 select_reduce_fusion
  10.0 0.1 fusion.17
  10.2 1.4 gather_fusion.2
  11.6 0.2 select_multiply_fusion.1
  11.8 1.1 reshape.100
  12.9 1.2 copy.16
  14.1 6.5 %all-to-all-start.1 = ((bf16[8,48,1792]{2,1,0:T(8,128)(2,1)}), bf16[8,48,1792]{2,1,0:T(8,128)(2,1)}, u32[]{:S(2)}, u32[]{:S(2)}) async-start(bf16[8,48,1792]{2,1,0:T(8,128)(2,1)} %bitcast.10), calls=%async_computation.1 | async-start | bytes 2752512 | tf_op jit(solution)/shard_map/all_to_all | solution.py:79
  20.6 1.4 gather_fusion.1
  22.1 0.4 multiply_convert_fusion
  22.6 1.1 reshape.97
  23.6 1.3 copy.15
  24.9 29.4 %all-to-all-done.1 = bf16[8,48,1792]{2,1,0:T(8,128)(2,1)} async-done(((bf16[8,48,1792]{2,1,0:T(8,128)(2,1)}), bf16[8,48,1792]{2,1,0:T(8,128)(2,1)}, u32[]{:S(2)}, u32[]{:S(2)}) %all-to-all-start.1) | async-done | bytes 1376288 | tf_op jit(solution)/shard_map/all_to_all | solution.py:79
  54.3 3.6 %all-to-all-start = ((bf16[8,48,1792]{2,1,0:T(8,128)(2,1)}), bf16[8,48,1792]{2,1,0:T(8,128)(2,1)S(1)}, u32[]{:S(2)}, u32[]{:S(2)}) async-start(bf16[8,48,1792]{2,1,0:T(8,128)(2,1)} %bitcast.5), calls=%async_computation | async-start | bytes 2752512 | tf_op jit(solution)/shard_map/all_to_all | solution.py:80
  57.8 0.2 reduce-scatter.2.cloned.1.call-start
  58.1 2.7 all-gather.8.cloned.1.call-done
  60.8 4.1 %convolution_convert_fusion.3 = bf16[384,1024]{1,0:T(8,128)(2,1)S(1)} fusion(bf16[384,1792]{1,0:T(8,128)(2,1)} %bitcast.11, bf16[1024,1792]{1,0:T(8,128)(2,1)} %all-gather.8.cloned.1.call-done), kind=kOutput, calls=%fused_computation.14 | convolution fusion | flops 1409679360 | bytes 5832704 | tf_op jit(solution)/shard_map/dot_general | solution.py:91
  64.9 0.8 dynamic-slice_bitcast_fusion
  65.7 1.5 collective-permute-start.4
  67.2 43.7 %all-gather.6.cloned.1.call-done = bf16[1024,1792]{1,0:T(8,128)(2,1)} async-done(((bf16[256,1792]{1,0:T(8,128)(2,1)}), bf16[1024,1792]{1,0:T(8,128)(2,1)}) %all-gather.6.cloned.1.call-update) | async-done | bytes 3670032 | tf_op jit(solution)/shard_map/all_gather | solution.py:87
  110.9 4.1 %convolution_convert_fusion.4 = bf16[384,1024]{1,0:T(8,128)(2,1)S(1)} fusion(bf16[384,1792]{1,0:T(8,128)(2,1)} %bitcast.11, bf16[1024,1792]{1,0:T(8,128)(2,1)} %all-gather.6.cloned.1.call-done), kind=kOutput, calls=%fused_computation.15 | convolution fusion | flops 1409679360 | bytes 5832704 | tf_op jit(solution)/shard_map/dot_general | solution.py:94
  115.0 0.8 dynamic-slice_bitcast_fusion.2
  115.8 1.5 collective-permute-start.2
  117.3 43.7 %all-gather.4.cloned.1.call-done = bf16[1024,1792]{1,0:T(8,128)(2,1)} async-done(((bf16[256,1792]{1,0:T(8,128)(2,1)}), bf16[1024,1792]{1,0:T(8,128)(2,1)}) %all-gather.4.cloned.1.call-update) | async-done | bytes 3670032 | tf_op jit(solution)/shard_map/all_gather | solution.py:88
  161.0 3.6 %convolution_convert_fusion.5 = bf16[384,1024]{1,0:T(8,128)(2,1)S(1)} fusion(bf16[384,1792]{1,0:T(8,128)(2,1)S(1)} %bitcast.52, bf16[1024,1792]{1,0:T(8,128)(2,1)} %all-gather.4.cloned.1.call-done), kind=kOutput, calls=%fused_computation.16 | convolution fusion | flops 1409679360 | bytes 5832704 | tf_op jit(solution)/shard_map/dot_general | solution.py:97
  164.7 0.8 dynamic-slice_bitcast_fusion.4
  165.5 1.5 collective-permute-start
  167.0 1.1 fusion.8
  168.1 1.1 fusion.10
  169.2 0.6 collective-permute-start.3
  169.8 6.7 %collective-permute-done = bf16[1,384,512]{2,1,0:T(8,128)(2,1)} collective-permute-done((bf16[1,384,512]{2,1,0:T(8,128)(2,1)}, bf16[1,384,512]{2,1,0:T(8,128)(2,1)}, u32[]{:S(2)}, u32[]{:S(2)}) %collective-permute-start) | collective-permute-done | bytes 393248 | tf_op jit(solution)/shard_map/ppermute | solution.py:26
  176.5 1.1 fusion.12
  177.9 1.5 collective-permute-done.1
  179.3 0.1 convert_reduce_fusion.2
  179.5 0.3 multiply_convert_fusion.1
  179.8 0.2 collective-permute-start.10
  180.0 0.4 collective-permute-start.6
  180.3 0.9 collective-permute-done.10
  181.4 1.6 collective-permute-start.11
  183.0 0.6 collective-permute-start.7
  183.6 0.7 collective-permute-done.8
  184.5 0.8 collective-permute-start.9
  185.3 8.2 %collective-permute-done.11 = bf16[384,512]{1,0:T(8,128)(2,1)} collective-permute-done((bf16[384,512]{1,0:T(8,128)(2,1)S(1)}, bf16[384,512]{1,0:T(8,128)(2,1)}, u32[]{:S(2)}, u32[]{:S(2)}) %collective-permute-start.11) | collective-permute-done | bytes 393248 | tf_op jit(solution)/shard_map/ppermute | solution.py:26
  193.5 3.3 convolution_convert_fusion
  196.8 5.1 %collective-permute-done.7 = bf16[384,512]{1,0:T(8,128)(2,1)S(1)} collective-permute-done((bf16[384,512]{1,0:T(8,128)(2,1)S(1)}, bf16[384,512]{1,0:T(8,128)(2,1)S(1)}, u32[]{:S(2)}, u32[]{:S(2)}) %collective-permute-start.7) | collective-permute-done | bytes 393248 | tf_op jit(solution)/shard_map/ppermute | solution.py:26
  201.8 3.5 %convolution_convert_fusion.2 = bf16[1024,1792]{1,0:T(8,128)(2,1)S(1)} fusion(bf16[384,1792]{1,0:T(8,128)(2,1)} %bitcast.11, bf16[384,512]{1,0:T(8,128)(2,1)S(1)} %collective-permute-done.7, bf16[384,512]{1,0:T(8,128)(2,1)S(1)} %maximum_select_fusion.4, pred[]{:T(512)S(6)} %eq.48), kind=kOutput, calls=%fused_computation.6 | convolution fusion | flops 1414660096 | bytes 5832705 | tf_op jit(solution)/shard_map/dot_general | solution.py:143
  205.3 4.1 %collective-permute-done.9 = bf16[384,512]{1,0:T(8,128)(2,1)S(1)} collective-permute-done((bf16[384,512]{1,0:T(8,128)(2,1)S(1)}, bf16[384,512]{1,0:T(8,128)(2,1)S(1)}, u32[]{:S(2)}, u32[]{:S(2)}) %collective-permute-start.9) | collective-permute-done | bytes 393248 | tf_op jit(solution)/shard_map/ppermute | solution.py:26
  209.4 0.7 copy-done.6
  210.2 3.4 %convolution_convert_fusion.1 = bf16[1024,1792]{1,0:T(8,128)(2,1)S(1)} fusion(bf16[384,1792]{1,0:T(8,128)(2,1)} %bitcast.11, bf16[384,512]{1,0:T(8,128)(2,1)S(1)} %collective-permute-done.9, bf16[384,512]{1,0:T(8,128)(2,1)S(1)} %maximum_select_fusion.5, pred[]{:T(512)S(6)} %eq.48), kind=kOutput, calls=%fused_computation.5 | convolution fusion | flops 1414660096 | bytes 5832705 | tf_op jit(solution)/shard_map/dot_general | solution.py:144
  213.6 5.9 %pad_maximum_fusion = bf16[1024,5376]{1,0:T(8,128)(2,1)} fusion(bf16[1024,1792]{1,0:T(8,128)(2,1)S(1)} %convolution_convert_fusion, bf16[1024,1792]{1,0:T(8,128)(2,1)S(1)} %convolution_convert_fusion.1, bf16[1024,1792]{1,0:T(8,128)(2,1)S(1)} %convolution_convert_fusion.2), kind=kLoop, calls=%fused_computation.3 | loop fusion | flops 33030144 | bytes 22020096 | tf_op jit(solution)/shard_map/concatenate | solution.py:147
  219.5 1.0 copy-done.7
  220.5 3.8 %fusion.14 = f32[384,1792]{1,0:T(8,128)S(1)} fusion(bf16[1024,1792]{1,0:T(8,128)(2,1)} %all-gather.6.cloned.1.call-done, bf16[384,512]{1,0:T(8,128)(2,1)S(1)} %copy-done.7, bf16[384,512]{1,0:T(8,128)(2,1)S(1)} %maximum_select_fusion.5, pred[]{:T(512)S(6)} %eq.48), kind=kOutput, calls=%fused_computation.59 | convolution fusion | flops 1412825088 | bytes 7208961 | tf_op jit(solution)/shard_map/dot_general | solution.py:141
  224.3 2.7 fusion
  227.0 4.6 %all-to-all-start.2 = ((bf16[8,48,1792]{2,1,0:T(8,128)(2,1)}), bf16[8,48,1792]{2,1,0:T(8,128)(2,1)S(1)}, u32[]{:S(2)}, u32[]{:S(2)}) async-start(bf16[8,48,1792]{2,1,0:T(8,128)(2,1)} %bitcast.16), calls=%async_computation.2 | async-start | bytes 2752512 | tf_op jit(solution)/shard_map/all_to_all | solution.py:155
  231.6 33.6 %all-to-all-done.2 = bf16[8,48,1792]{2,1,0:T(8,128)(2,1)S(1)} async-done(((bf16[8,48,1792]{2,1,0:T(8,128)(2,1)}), bf16[8,48,1792]{2,1,0:T(8,128)(2,1)S(1)}, u32[]{:S(2)}, u32[]{:S(2)}) %all-to-all-start.2) | async-done | bytes 1376288 | tf_op jit(solution)/shard_map/all_to_all | solution.py:155
  265.2 0.7 copy.17
  265.9 0.2 copy.18
  266.1 2.9 gather_fusion
  269.0 3.1 select_multiply_fusion
  272.1 55.3 %reduce-scatter.2.cloned.1.call-done = bf16[256,5376]{1,0:T(8,128)(2,1)} async-done(((bf16[1024,5376]{1,0:T(8,128)(2,1)}), bf16[256,5376]{1,0:T(8,128)(2,1)}) %reduce-scatter.2.cloned.1.call-update) | async-done | bytes 2752528 | tf_op jit(solution)/shard_map/reduce_scatter | solution.py:146
  327.4 3.3 fusion.24
  (43 shorter events, 1.2 us)
Async XLA Ops:
  7.2 3.0 copy-start
  7.2 2.2 copy-start.3
  7.2 53.6 %all-gather.8.cloned.1.call-start = ((), (), s32[]{:S(2)}) async-start(), calls=%async_computation.6 | async-start | bytes 4587520 | tf_op jit(solution)/shard_map/all_gather | solution.py:86
  7.9 103.0 %all-gather.6.cloned.1.call-start = ((), (), s32[]{:S(2)}) async-start(), calls=%async_computation.5 | async-start | bytes 4587520 | tf_op jit(solution)/shard_map/all_gather | solution.py:87
  8.7 152.3 %all-gather.4.cloned.1.call-start = ((), (), s32[]{:S(2)}) async-start(), calls=%async_computation.4 | async-start | bytes 4587520 | tf_op jit(solution)/shard_map/all_gather | solution.py:88
  14.1 6.5 %copy-start.2 = (bf16[128,7168]{1,0:T(8,128)(2,1)S(1)}, bf16[128,7168]{1,0:T(8,128)(2,1)}, u32[]{:S(2)}) copy-start(bf16[128,7168]{1,0:T(8,128)(2,1)} %param.10) | copy-start | bytes 5505028
  14.1 40.2 %all-to-all-start.1 = ((bf16[8,48,1792]{2,1,0:T(8,128)(2,1)}), bf16[8,48,1792]{2,1,0:T(8,128)(2,1)}, u32[]{:S(2)}, u32[]{:S(2)}) async-start(bf16[8,48,1792]{2,1,0:T(8,128)(2,1)} %bitcast.10), calls=%async_computation.1 | async-start | bytes 2752512 | tf_op jit(solution)/shard_map/all_to_all | solution.py:79
  20.6 1.4 copy-start.4
  54.3 63.0 %all-to-all-start = ((bf16[8,48,1792]{2,1,0:T(8,128)(2,1)}), bf16[8,48,1792]{2,1,0:T(8,128)(2,1)S(1)}, u32[]{:S(2)}, u32[]{:S(2)}) async-start(bf16[8,48,1792]{2,1,0:T(8,128)(2,1)} %bitcast.5), calls=%async_computation | async-start | bytes 2752512 | tf_op jit(solution)/shard_map/all_to_all | solution.py:80
  57.8 269.6 %reduce-scatter.2.cloned.1.call-start = ((), (), s32[]{:S(2)}) async-start(), calls=%async_computation.7 | async-start | bytes 13762560 | tf_op jit(solution)/shard_map/reduce_scatter | solution.py:146
  65.7 101.3 %collective-permute-start.4 = (bf16[1,384,512]{2,1,0:T(8,128)(2,1)}, bf16[1,384,512]{2,1,0:T(8,128)(2,1)}, u32[]{:S(2)}, u32[]{:S(2)}) collective-permute-start(bf16[1,384,512]{2,1,0:T(8,128)(2,1)} %get-tuple-element.19), channel_id=1, source_target_pairs={{0,2},{1,3},{2,0},{3,1},{4,6},{5,7},{6,4},{7,5},{8,10},{9,11},{10,... | collective-permute-start | bytes 1179656 | tf_op jit(solution)/shard_map/ppermute | solution.py:26
  115.8 52.3 %collective-permute-start.2 = (bf16[1,384,512]{2,1,0:T(8,128)(2,1)}, bf16[1,384,512]{2,1,0:T(8,128)(2,1)}, u32[]{:S(2)}, u32[]{:S(2)}) collective-permute-start(bf16[1,384,512]{2,1,0:T(8,128)(2,1)} %get-tuple-element.15), channel_id=1, source_target_pairs={{0,2},{1,3},{2,0},{3,1},{4,6},{5,7},{6,4},{7,5},{8,10},{9,11},{10,... | collective-permute-start | bytes 1179656 | tf_op jit(solution)/shard_map/ppermute | solution.py:26
  165.5 11.0 %collective-permute-start = (bf16[1,384,512]{2,1,0:T(8,128)(2,1)}, bf16[1,384,512]{2,1,0:T(8,128)(2,1)}, u32[]{:S(2)}, u32[]{:S(2)}) collective-permute-start(bf16[1,384,512]{2,1,0:T(8,128)(2,1)} %get-tuple-element.23), channel_id=1, source_target_pairs={{0,2},{1,3},{2,0},{3,1},{4,6},{5,7},{6,4},{7,5},{8,10},{9,11},{10,... | collective-permute-start | bytes 1179656 | tf_op jit(solution)/shard_map/ppermute | solution.py:26
  168.0 9.6 %collective-permute-start.5 = (bf16[2,384,256]{2,1,0:T(8,128)(2,1)S(1)}, bf16[2,384,256]{2,1,0:T(8,128)(2,1)S(1)}, u32[]{:S(2)}, u32[]{:S(2)}) collective-permute-start(bf16[2,384,256]{2,1,0:T(8,128)(2,1)S(1)} %get-tuple-element.18), channel_id=1, source_target_pairs={{0,1},{1,0},{2,3},{3,2},{4,5},{5,4},{6,7},{7,6},{8,9},{9,8},{10,11... | collective-permute-start | bytes 1179656 | tf_op jit(solution)/shard_map/ppermute | solution.py:26
  169.2 8.5 %collective-permute-start.3 = (bf16[2,384,256]{2,1,0:T(8,128)(2,1)S(1)}, bf16[2,384,256]{2,1,0:T(8,128)(2,1)S(1)}, u32[]{:S(2)}, u32[]{:S(2)}) collective-permute-start(bf16[2,384,256]{2,1,0:T(8,128)(2,1)S(1)} %get-tuple-element.14), channel_id=1, source_target_pairs={{0,1},{1,0},{2,3},{3,2},{4,5},{5,4},{6,7},{7,6},{8,9},{9,8},{10,11... | collective-permute-start | bytes 1179656 | tf_op jit(solution)/shard_map/ppermute | solution.py:26
  177.6 1.8 collective-permute-start.1
  179.8 1.5 collective-permute-start.10
  180.0 3.0 collective-permute-start.6
  181.4 12.2 %collective-permute-start.11 = (bf16[384,512]{1,0:T(8,128)(2,1)S(1)}, bf16[384,512]{1,0:T(8,128)(2,1)}, u32[]{:S(2)}, u32[]{:S(2)}) collective-permute-start(bf16[384,512]{1,0:T(8,128)(2,1)S(1)} %maximum_select_fusion.6), channel_id=1, source_target_pairs={{0,2},{1,3},{2,0},{3,1},{4,6},{5,7},{6,4},{7,5},{8,10},{9,11},{10,... | collective-permute-start | bytes 1179656 | tf_op jit(solution)/shard_map/ppermute | solution.py:26
  182.9 1.4 collective-permute-start.8
  183.0 18.8 %collective-permute-start.7 = (bf16[384,512]{1,0:T(8,128)(2,1)S(1)}, bf16[384,512]{1,0:T(8,128)(2,1)S(1)}, u32[]{:S(2)}, u32[]{:S(2)}) collective-permute-start(bf16[384,512]{1,0:T(8,128)(2,1)S(1)} %maximum_select_fusion.4), channel_id=1, source_target_pairs={{0,2},{1,3},{2,0},{3,1},{4,6},{5,7},{6,4},{7,5},{8,10},{9,11},{10,... | collective-permute-start | bytes 1179656 | tf_op jit(solution)/shard_map/ppermute | solution.py:26
  184.5 25.0 %collective-permute-start.9 = (bf16[384,512]{1,0:T(8,128)(2,1)S(1)}, bf16[384,512]{1,0:T(8,128)(2,1)S(1)}, u32[]{:S(2)}, u32[]{:S(2)}) collective-permute-start(bf16[384,512]{1,0:T(8,128)(2,1)S(1)} %maximum_select_fusion.5), channel_id=1, source_target_pairs={{0,2},{1,3},{2,0},{3,1},{4,6},{5,7},{6,4},{7,5},{8,10},{9,11},{10,... | collective-permute-start | bytes 1179656 | tf_op jit(solution)/shard_map/ppermute | solution.py:26
  209.4 0.7 copy-start.6
  219.5 1.0 copy-start.7
  220.5 3.8 %copy-start.5 = (bf16[1024,1792]{1,0:T(8,128)(2,1)S(1)}, bf16[1024,1792]{1,0:T(8,128)(2,1)}, u32[]{:S(2)}) copy-start(bf16[1024,1792]{1,0:T(8,128)(2,1)} %all-gather.8.cloned.1.call-done) | copy-start | bytes 11010052
  227.0 38.2 %all-to-all-start.2 = ((bf16[8,48,1792]{2,1,0:T(8,128)(2,1)}), bf16[8,48,1792]{2,1,0:T(8,128)(2,1)S(1)}, u32[]{:S(2)}, u32[]{:S(2)}) async-start(bf16[8,48,1792]{2,1,0:T(8,128)(2,1)} %bitcast.16), calls=%async_computation.2 | async-start | bytes 2752512 | tf_op jit(solution)/shard_map/all_to_all | solution.py:155
  269.0 61.8 %copy-start.1 = (bf16[128,7168]{1,0:T(8,128)(2,1)S(1)}, bf16[128,7168]{1,0:T(8,128)(2,1)}, u32[]{:S(2)}) copy-start(bf16[128,7168]{1,0:T(8,128)(2,1)} %param.9) | copy-start | bytes 5505028
Sparse Core Ops, SparseCore 0:
  9.8 50.9 all-gather.7
  62.7 48.1 all-gather.5
  112.8 48.1 all-gather.3
  219.7 107.7 reduce-scatter.1
where the time goes:
time: 338 us; the launch traced here: 337 us
  waiting for transfers between devices  238 us (70%)
  matrix products  28.4 us (8%)
  starting transfers between devices  23.7 us (7%)
  local copies, waits for them, and re-layouts  18.8 us (6%)
  other arithmetic  14.5 us (4%)
  between operations  14.2 us (4%)
    reduce_scatter x1, waiting for transfers between devices, body(): lax.psum_scatter(jnp.concatenate([gate_term, up_term, down_term], axis=1)...  55.3 us
    all_gather x1, waiting for transfers between devices, body(): lax.all_gather(w_down, 'dp', axis=0, tiled=True)  43.7 us
    all_gather x1, waiting for transfers between devices, body(): lax.all_gather(w_up, 'dp', axis=0, tiled=True)  43.7 us
    all_to_all x1, waiting for transfers between devices, body(): lax.all_to_all(expert_dx.reshape(devices_ep, capacity, quarter), 'ep', sp...  33.6 us
    all_to_all x1, waiting for transfers between devices, body(): lax.all_to_all(x_send, 'ep', split_axis=0, concat_axis=0, tiled=True)  29.4 us
    ppermute x12, waiting for transfers between devices, from_partner(): return lax.ppermute(value, axis, pairs)  27.3 us
    ppermute x12, starting transfers between devices, from_partner(): return lax.ppermute(value, axis, pairs)  8.71 us
  transfers between devices with their start and end apart: 19, of which 13 were waited for; matrix products, arithmetic and copies ran while one was open for 14% of the time, Pallas kernels for 0%

commit v1 on v0

v1 whole, which is shorter than its diff:
```python
import jax
import jax.numpy as jnp
from jax import lax
from jax.sharding import PartitionSpec as P

D = 7168
GROUP = 4
TOP = 1


CONTRACT_LAST = (((1,), (1,)), ((), ()))
CONTRACT_FIRST = (((0,), (0,)), ((), ()))


def as_sent(value):

    def short(part):
        return part.astype(jnp.bfloat16) if part.dtype == jnp.float32 else part

    return jax.tree.map(short, value)


def from_partner(value, axis, distance):
    mask = 2**distance
    pairs = [(source, source ^ mask) for source in range(lax.axis_size(axis))]
    return lax.ppermute(value, axis, pairs)


def slot_tables(expert_ids, route_weight, experts, capacity):
    token_count, top_count = expert_ids.shape
    pair_count = token_count * top_count
    flat_ids = expert_ids.reshape(pair_count)
    onehot = (flat_ids[:, None] == jnp.arange(experts, dtype=jnp.int32)[None, :]).astype(jnp.int32)
    before = jnp.cumsum(onehot, axis=0) - onehot
    ranks = jnp.sum(before * onehot, axis=1)
    kept = ranks < capacity
    slots = jnp.where(kept, flat_ids * capacity + ranks, 0)
    slot_ids = jnp.arange(experts * capacity, dtype=jnp.int32)
    match = (slots[None, :] == slot_ids[:, None]) & kept[None, :]
    pair_ids = jnp.arange(pair_count, dtype=jnp.int32)
    pair_of_slot = jnp.sum(jnp.where(match, pair_ids[None, :], 0), axis=1)
    filled = jnp.any(match, axis=1)
    flat_weight = route_weight.reshape(pair_count)
    weight_of_slot = jnp.sum(jnp.where(match, flat_weight[None, :], jnp.float32(0.0)), axis=1)
    return (kept, slots, pair_of_slot // top_count, filled, weight_of_slot)


def activations(gate, up, back):
    logistic = jax.nn.sigmoid(gate)
    silu = gate * logistic
    hidden = (silu * up).astype(jnp.bfloat16)
    d_gate = (back * up * logistic * (1.0 + gate * (1.0 - logistic))).astype(jnp.bfloat16)
    d_up = (back * silu).astype(jnp.bfloat16)
    return (hidden, d_gate, d_up)


def swap(value, axis, distance):
    return from_partner(value, axis, distance)


def wide(value):
    return value.astype(jnp.float32)


def dot_last(left, right):
    return lax.dot_general(left, right, CONTRACT_LAST, preferred_element_type=jnp.float32)


def dot_first(left, right):
    return lax.dot_general(left, right, CONTRACT_FIRST, preferred_element_type=jnp.float32)


def body(tokens, out_grad, route_weight, expert_ids, w_gate, w_up, w_down):
    devices_ep = lax.axis_size("ep")
    experts = devices_ep // GROUP
    token_count = tokens.shape[0]
    capacity = 6 * GROUP * token_count * TOP // (8 * devices_ep)
    quarter = D // GROUP
    short = jnp.bfloat16
    kept, slots, token_of_slot, filled, weight_of_slot = slot_tables(
        expert_ids, route_weight, experts, capacity
    )
    other_w = tuple(swap(w, "dp", 1) for w in (w_gate, w_up, w_down))
    token_ids = jnp.arange(token_count, dtype=jnp.int32)
    pick = ((token_of_slot[:, None] == token_ids[None, :]) & filled[:, None]).astype(short)
    x_slots = jnp.dot(pick, tokens, preferred_element_type=jnp.float32).astype(short)
    d_slots = (
        jnp.dot(pick, out_grad, preferred_element_type=jnp.float32) * weight_of_slot[:, None]
    ).astype(short)

    def to_owners(rows):
        shaped = rows.reshape(experts, capacity, GROUP, quarter).transpose(0, 2, 1, 3)
        return shaped.reshape(devices_ep, capacity, quarter)

    def sent(rows):
        return lax.all_to_all(to_owners(rows), "ep", split_axis=0, concat_axis=0, tiled=True)

    row_count = devices_ep * capacity
    x_own = sent(x_slots).reshape(row_count, quarter)
    d_own = sent(d_slots).reshape(row_count, quarter)
    x_other, d_other = swap(x_own, "dp", 0), swap(d_own, "dp", 0)
    core = lax.axis_index("ep") % 2
    weights = ((w_gate, w_up, w_down), other_w)
    acts = []
    for x_rows, d_rows in ((x_own, d_own), (x_other, d_other)):
        terms = [
            jnp.concatenate(
                [dot_last(x_rows, wg), dot_last(x_rows, wu), dot_last(d_rows, wd)], axis=1
            ).astype(short)
            for wg, wu, wd in weights
        ]
        give = jnp.where(core == 0, terms[1], terms[0])
        keep = jnp.where(core == 0, terms[0], terms[1])
        pair = (wide(keep) + wide(swap(give, "ep", 0))).astype(short)
        total = wide(pair) + wide(swap(pair, "ep", 1))
        width = total.shape[1] // 3
        mine = jnp.concatenate(
            activations(total[:, :width], total[:, width : 2 * width], total[:, 2 * width :]), axis=1
        )
        theirs = swap(mine, "ep", 0)
        first = jnp.where(core == 0, mine, theirs)
        second = jnp.where(core == 0, theirs, mine)
        acts.append(
            tuple(
                tuple(half[:, piece * width : (piece + 1) * width] for piece in range(3))
                for half in (first, second)
            )
        )

    def grads(half):
        (h0, g0, u0), (h1, g1, u1) = acts[0][half], acts[1][half]
        return (
            dot_first(g0, x_own) + dot_first(g1, x_other),
            dot_first(u0, x_own) + dot_first(u1, x_other),
            dot_first(h0, d_own) + dot_first(h1, d_other),
        )

    def dx(rows):
        return sum(
            jnp.dot(acts[rows][half][1], weights[half][0], preferred_element_type=jnp.float32)
            + jnp.dot(acts[rows][half][2], weights[half][1], preferred_element_type=jnp.float32)
            for half in range(2)
        )

    dx_in = swap(dx(1).astype(short), "dp", 0)
    away = tuple(swap(term.astype(short), "dp", 1) for term in grads(1))
    expert_dx = (dx(0) + wide(dx_in)).astype(short)
    grad_gate, grad_up, grad_down = (
        (own + wide(term)).astype(short) for own, term in zip(grads(0), away)
    )
    returned = lax.all_to_all(
        expert_dx.reshape(devices_ep, capacity, quarter),
        "ep",
        split_axis=0,
        concat_axis=0,
        tiled=True,
    )
    slot_rows = (
        returned.reshape(experts, GROUP, capacity, quarter)
        .transpose(0, 2, 1, 3)
        .reshape(experts * capacity, D)
    )
    in_grad = dot_first(pick, slot_rows).astype(short)
    return (in_grad, grad_gate, grad_up, grad_down)


def solution(mesh):
    placed = (
        P(("dp", "ep"), None),
        P(("dp", "ep"), None),
        P(("dp", "ep"), None),
        P(("dp", "ep"), None),
        P("dp", "ep"),
        P("dp", "ep"),
        P("dp", "ep"),
    )
    return jax.shard_map(
        body,
        mesh=mesh,
        in_specs=placed,
        out_specs=(P(("dp", "ep"), None), P("dp", "ep"), P("dp", "ep"), P("dp", "ep")),
        check_vma=False,
    )
```

time: 338 us -> 270 us (0.80)
  waiting for transfers between devices: 238 us -> 157 us
  matrix products: 28.4 us -> 62.3 us
  between operations: 14.2 us -> 1.1 us
  other arithmetic: 14.5 us -> 4.94 us
  starting transfers between devices: 23.7 us -> 31.7 us
  local copies, waits for them, and re-layouts: 18.8 us -> 11.3 us
    all_gather x3 -> x0, waiting for transfers between devices: 90.1 us -> none  [the longest x1 43.7 us: body(): lax.all_gather(w_down, 'dp', axis=0, tiled=True)]
    ppermute x12 -> x15, waiting for transfers between devices: 27.3 us -> 102 us  [from_partner(): return lax.ppermute(value, axis, pairs)]
    reduce_scatter x1 -> x0, waiting for transfers between devices: 55.3 us -> none  [body(): lax.psum_scatter(jnp.concatenate([gate_term, up_term, down_term], axis=1)...]
    dot_general x8 -> x35, matrix products: 28.4 us -> 62.3 us  [the longest x12 23.3 us: dot_last(): lax.dot_general(left, right, CONTRACT_LAST, preferred_element_type=jnp.fl...]
    all_to_all x1, waiting for transfers between devices: 33.6 us -> 3.55 us  [body(): lax.all_to_all(expert_dx.reshape(devices_ep, capacity, quarter), 'ep', sp...]
    all_to_all x2, waiting for transfers between devices: 29.4 us -> 51.5 us  [sent(): lax.all_to_all(to_owners(rows), 'ep', split_axis=0, concat_axis=0, tiled=...]
    concatenate x4 -> x2, other arithmetic: 9.1 us -> 0.12 us  [body(): jnp.concatenate(activations(total[:, :width], total[:, width:2 * width],...]
    ppermute x12 -> x15, starting transfers between devices: 8.71 us -> 16 us  [from_partner(): return lax.ppermute(value, axis, pairs)]
  transfers between devices with their start and end apart: 19 -> 18, of which waited for: 13 -> 11; matrix products, arithmetic and copies ran while one was open for 14% -> 21% of each run, Pallas kernels for 0% -> 0%
where the time goes in v1:
time: 270 us; the launch traced here: 268 us
  waiting for transfers between devices  157 us (58%)
  matrix products  62.3 us (23%)
  starting transfers between devices  31.7 us (12%)
  local copies, waits for them, and re-layouts  11.3 us (4%)
  other arithmetic  4.94 us (2%)
    ppermute x15, waiting for transfers between devices, from_partner(): return lax.ppermute(value, axis, pairs)  102 us
    all_to_all x2, waiting for transfers between devices, sent(): lax.all_to_all(to_owners(rows), 'ep', split_axis=0, concat_axis=0, tiled=...  51.5 us
    dot_general x12, matrix products, dot_last(): lax.dot_general(left, right, CONTRACT_LAST, preferred_element_type=jnp.fl...  23.3 us
    dot_general x13, matrix products, dot_first(): lax.dot_general(left, right, CONTRACT_FIRST, preferred_element_type=jnp.f...  19.5 us
    ppermute x15, starting transfers between devices, from_partner(): return lax.ppermute(value, axis, pairs)  16 us
    all_to_all x2, starting transfers between devices, sent(): lax.all_to_all(to_owners(rows), 'ep', split_axis=0, concat_axis=0, tiled=...  10.9 us
    reshape x4, local copies, waits for them, and re-layouts, to_owners(): rows.reshape(experts, capacity, GROUP, quarter).transpose(0, 2, 1, 3)  8.64 us
    dot_general x4, matrix products, dx(): jnp.dot(acts[rows][half][1], weights[half][0], preferred_element_type=jnp...  8.27 us
  transfers between devices with their start and end apart: 18, of which 11 were waited for; matrix products, arithmetic and copies ran while one was open for 21% of the time, Pallas kernels for 0%

profile of v1, /device:TPU:0, one launch (start us, length us, event | category | flops | bytes accessed | tf_op | source)
XLA Modules:
  0.0 268.5 jit_solution(2034710086149230066)
XLA Ops:
  0.6 0.9 fusion.47
  1.7 0.8 select_reduce_fusion
  2.5 0.7 add_select_fusion
  3.4 1.7 convolution_convert_fusion.1
  5.1 2.9 %reshape.53 = bf16[2,48,4,1792]{3,2,1,0:T(4,128)(2,1)S(1)} reshape(bf16[96,7168]{1,0:T(8,128)(2,1)} %convolution_convert_fusion.1) | data formatting | bytes 2752512 | tf_op jit(solution)/shard_map/reshape | solution.py:92
  8.1 1.2 copy.16
  9.3 6.5 %all-to-all-start = ((bf16[8,48,1792]{2,1,0:T(8,128)(2,1)}), bf16[8,48,1792]{2,1,0:T(8,128)(2,1)S(1)}, u32[]{:S(2)}, u32[]{:S(2)}) async-start(bf16[8,48,1792]{2,1,0:T(8,128)(2,1)} %bitcast.2), calls=%async_computation | async-start | bytes 2752512 | tf_op jit(solution)/shard_map/all_to_all | solution.py:96
  15.9 2.1 fusion
  18.0 1.9 reshape.56
  19.9 2.6 copy.17
  22.4 26.9 %all-to-all-done = bf16[8,48,1792]{2,1,0:T(8,128)(2,1)S(1)} async-done(((bf16[8,48,1792]{2,1,0:T(8,128)(2,1)}), bf16[8,48,1792]{2,1,0:T(8,128)(2,1)S(1)}, u32[]{:S(2)}, u32[]{:S(2)}) %all-to-all-start) | async-done | bytes 1376288 | tf_op jit(solution)/shard_map/all_to_all | solution.py:96
  49.3 4.4 %all-to-all-start.1 = ((bf16[8,48,1792]{2,1,0:T(8,128)(2,1)}), bf16[8,48,1792]{2,1,0:T(8,128)(2,1)}, u32[]{:S(2)}, u32[]{:S(2)}) async-start(bf16[8,48,1792]{2,1,0:T(8,128)(2,1)} %bitcast.6), calls=%async_computation.1 | async-start | bytes 2752512 | tf_op jit(solution)/shard_map/all_to_all | solution.py:96
  53.8 1.6 collective-permute-start.2
  55.9 1.5 collective-permute-start
  57.4 1.5 collective-permute-start.6
  58.9 1.8 convolution_convert_fusion.12
  60.7 1.8 convolution_convert_fusion.13
  62.6 24.6 %all-to-all-done.1 = bf16[8,48,1792]{2,1,0:T(8,128)(2,1)} async-done(((bf16[8,48,1792]{2,1,0:T(8,128)(2,1)}), bf16[8,48,1792]{2,1,0:T(8,128)(2,1)}, u32[]{:S(2)}, u32[]{:S(2)}) %all-to-all-start.1) | async-done | bytes 1376288 | tf_op jit(solution)/shard_map/all_to_all | solution.py:96
  87.2 2.2 convolution_convert_fusion.11
  89.5 2.2 convolution_convert_fusion.8
  91.7 24.2 %collective-permute-done = bf16[256,1792]{1,0:T(8,128)(2,1)} collective-permute-done((bf16[256,1792]{1,0:T(8,128)(2,1)}, bf16[256,1792]{1,0:T(8,128)(2,1)}, u32[]{:S(2)}, u32[]{:S(2)}) %collective-permute-start) | collective-permute-done | bytes 917536 | tf_op jit(solution)/shard_map/ppermute | solution.py:26
  115.9 1.8 convolution_convert_fusion.10
  117.7 1.8 convolution_convert_fusion.9
  119.8 1.6 collective-permute-start.7
  122.0 1.7 collective-permute-start.4
  123.8 1.8 convolution_convert_fusion.3
  125.6 1.8 convolution_convert_fusion.4
  127.4 25.2 %collective-permute-done.7 = bf16[384,1792]{1,0:T(8,128)(2,1)S(1)} collective-permute-done((bf16[384,1792]{1,0:T(8,128)(2,1)}, bf16[384,1792]{1,0:T(8,128)(2,1)S(1)}, u32[]{:S(2)}, u32[]{:S(2)}) %collective-permute-start.7) | collective-permute-done | bytes 1376288 | tf_op jit(solution)/shard_map/ppermute | solution.py:26
  152.6 2.3 convolution_convert_fusion.2
  155.0 1.8 convolution_convert_fusion.5
  156.8 1.8 convolution_convert_fusion.6
  158.6 1.8 convolution_convert_fusion.7
  161.7 1.0 collective-permute-done.8
  162.9 1.7 collective-permute-start.9
  164.9 13.5 %collective-permute-done.9 = bf16[384,768]{0,1:T(8,128)(2,1)S(1)} collective-permute-done((bf16[384,768]{0,1:T(8,128)(2,1)S(1)}, bf16[384,768]{0,1:T(8,128)(2,1)S(1)}, u32[]{:S(2)}, u32[]{:S(2)}) %collective-permute-start.9) | collective-permute-done | bytes 589856 | tf_op jit(solution)/shard_map/ppermute | solution.py:26
  178.9 1.8 fusion.38
  180.6 1.8 convolution_add_fusion.2
  182.7 2.2 fusion.32
  184.9 1.8 fusion.25
  186.6 1.8 convolution_add_fusion
  188.4 1.8 fusion.4
  190.2 1.6 collective-permute-start.11
  191.8 1.8 fusion.43
  193.6 0.6 fusion.17
  194.2 2.9 %fusion.14 = bf16[256,1792]{1,0:T(8,128)(2,1)} fusion(f32[256,1792]{1,0:T(8,128)S(1)} %fusion.17, bf16[384,1792]{1,0:T(8,128)(2,1)} %bitcast.7, bf16[384,768]{0,1:T(8,128)(2,1)S(1)} %get-tuple-element.10), kind=kOutput, calls=%fused_computation.27 | convolution fusion | flops 353239040 | bytes 4325376 | tf_op jit(solution)/shard_map/dot_general | solution.py:70
  197.1 1.5 collective-permute-start.14
  198.6 0.6 fusion.23
  199.3 1.6 fusion.13
  201.4 21.5 %collective-permute-done.11 = bf16[384,1792]{1,0:T(8,128)(2,1)S(1)} collective-permute-done((bf16[384,1792]{1,0:T(8,128)(2,1)S(1)}, bf16[384,1792]{1,0:T(8,128)(2,1)S(1)}, u32[]{:S(2)}, u32[]{:S(2)}) %collective-permute-start.11) | collective-permute-done | bytes 1376288 | tf_op jit(solution)/shard_map/ppermute | solution.py:26
  222.9 3.0 %fusion.5 = bf16[384,1792]{1,0:T(8,128)(2,1)} fusion(f32[384,1792]{1,0:T(8,128)S(1)} %convolution_add_fusion.2, f32[384,1792]{1,0:T(8,128)S(1)} %fusion.43, bf16[256,1792]{1,0:T(8,128)(2,1)} %param.11, bf16[384,1792]{1,0:T(8,128)(2,1)S(1)} %collective-permute-done.11, bf16[384,768]{0,1:T(8,128)(2,1)S(1)} %get-tuple-element.9), kind=kOutput, calls=%fused_computation.12 | convolution fusion | flops 355762176 | bytes 9371648 | tf_op jit(solution)/shard_map/dot_general | solution.py:140
  225.8 4.7 %all-to-all-start.2 = ((bf16[8,48,1792]{2,1,0:T(8,128)(2,1)}), bf16[8,48,1792]{2,1,0:T(8,128)(2,1)}, u32[]{:S(2)}, u32[]{:S(2)}) async-start(bf16[8,48,1792]{2,1,0:T(8,128)(2,1)} %bitcast.74), calls=%async_computation.2 | async-start | bytes 2752512 | tf_op jit(solution)/shard_map/all_to_all | solution.py:151
  230.6 1.6 fusion.27
  232.1 0.7 fusion.12
  232.8 1.6 collective-permute-start.12
  234.4 0.6 fusion.20
  235.0 0.6 fusion.30
  235.7 0.6 fusion.34
  236.8 3.2 %fusion.11 = bf16[256,1792]{1,0:T(8,128)(2,1)} fusion(f32[256,1792]{1,0:T(8,128)S(1)} %fusion.20, bf16[384,1792]{1,0:T(8,128)(2,1)} %bitcast.7, bf16[256,1792]{1,0:T(8,128)(2,1)} %collective-permute-done.14, bf16[384,768]{0,1:T(8,128)(2,1)S(1)} %copy-done.5), kind=kOutput, calls=%fused_computation.24 | convolution fusion | flops 354156544 | bytes 5242880 | tf_op jit(solution)/shard_map/dot_general | solution.py:70
  240.3 2.8 %fusion.10 = bf16[256,1792]{1,0:T(8,128)(2,1)} fusion(f32[256,1792]{1,0:T(8,128)S(1)} %fusion.30, bf16[384,1792]{1,0:T(8,128)(2,1)S(1)} %bitcast.72, bf16[256,1792]{1,0:T(8,128)(2,1)} %collective-permute-done.13, bf16[384,768]{0,1:T(8,128)(2,1)S(1)} %copy-done.5), kind=kOutput, calls=%fused_computation.23 | convolution fusion | flops 354156544 | bytes 5242880 | tf_op jit(solution)/shard_map/dot_general | solution.py:70
  243.1 16.0 %collective-permute-done.12 = bf16[256,1792]{1,0:T(8,128)(2,1)S(1)} collective-permute-done((bf16[256,1792]{1,0:T(8,128)(2,1)S(1)}, bf16[256,1792]{1,0:T(8,128)(2,1)S(1)}, u32[]{:S(2)}, u32[]{:S(2)}) %collective-permute-start.12) | collective-permute-done | bytes 917536 | tf_op jit(solution)/shard_map/ppermute | solution.py:26
  259.1 1.6 fusion.9
  260.7 3.5 %all-to-all-done.2 = bf16[8,48,1792]{2,1,0:T(8,128)(2,1)} async-done(((bf16[8,48,1792]{2,1,0:T(8,128)(2,1)}), bf16[8,48,1792]{2,1,0:T(8,128)(2,1)}, u32[]{:S(2)}, u32[]{:S(2)}) %all-to-all-start.2) | async-done | bytes 1376288 | tf_op jit(solution)/shard_map/all_to_all | solution.py:151
  264.2 2.0 copy.18
  266.5 2.0 convolution_convert_fusion
  (53 shorter events, 5.8 us)
Async XLA Ops:
  0.6 2.8 %copy-start = (bf16[128,7168]{1,0:T(8,128)(2,1)S(1)}, bf16[128,7168]{1,0:T(8,128)(2,1)}, u32[]{:S(2)}) copy-start(bf16[128,7168]{1,0:T(8,128)(2,1)} %param.7) | copy-start | bytes 5505028
  9.3 6.5 %copy-start.9 = (f32[128,1]{0,1:T(1,128)S(1)}, f32[128,1]{0,1:T(1,128)}, u32[]{:S(2)}) copy-start(f32[128,1]{0,1:T(1,128)} %param.9) | copy-start | bytes 1540
  9.3 40.1 %all-to-all-start = ((bf16[8,48,1792]{2,1,0:T(8,128)(2,1)}), bf16[8,48,1792]{2,1,0:T(8,128)(2,1)S(1)}, u32[]{:S(2)}, u32[]{:S(2)}) async-start(bf16[8,48,1792]{2,1,0:T(8,128)(2,1)} %bitcast.2), calls=%async_computation | async-start | bytes 2752512 | tf_op jit(solution)/shard_map/all_to_all | solution.py:96
  49.3 37.9 %all-to-all-start.1 = ((bf16[8,48,1792]{2,1,0:T(8,128)(2,1)}), bf16[8,48,1792]{2,1,0:T(8,128)(2,1)}, u32[]{:S(2)}, u32[]{:S(2)}) async-start(bf16[8,48,1792]{2,1,0:T(8,128)(2,1)} %bitcast.6), calls=%async_computation.1 | async-start | bytes 2752512 | tf_op jit(solution)/shard_map/all_to_all | solution.py:96
  53.8 35.7 %collective-permute-start.2 = (bf16[256,1792]{1,0:T(8,128)(2,1)}, bf16[256,1792]{1,0:T(8,128)(2,1)}, u32[]{:S(2)}, u32[]{:S(2)}) collective-permute-start(bf16[256,1792]{1,0:T(8,128)(2,1)} %param.13), channel_id=1, source_target_pairs={{0,16},{8,24},{16,0},{24,8},{1,17},{9,25},{17,1},{25,9},{2,18},{10... | collective-permute-start | bytes 2752520 | tf_op jit(solution)/shard_map/ppermute | solution.py:26
  55.4 62.3 %collective-permute-start.1 = (bf16[256,1792]{1,0:T(8,128)(2,1)}, bf16[256,1792]{1,0:T(8,128)(2,1)}, u32[]{:S(2)}, u32[]{:S(2)}) collective-permute-start(bf16[256,1792]{1,0:T(8,128)(2,1)} %param.12), channel_id=1, source_target_pairs={{0,16},{8,24},{16,0},{24,8},{1,17},{9,25},{17,1},{25,9},{2,18},{10... | collective-permute-start | bytes 2752520 | tf_op jit(solution)/shard_map/ppermute | solution.py:26
  55.9 60.0 %collective-permute-start = (bf16[256,1792]{1,0:T(8,128)(2,1)}, bf16[256,1792]{1,0:T(8,128)(2,1)}, u32[]{:S(2)}, u32[]{:S(2)}) collective-permute-start(bf16[256,1792]{1,0:T(8,128)(2,1)} %param.11), channel_id=1, source_target_pairs={{0,16},{8,24},{16,0},{24,8},{1,17},{9,25},{17,1},{25,9},{2,18},{10... | collective-permute-start | bytes 2752520 | tf_op jit(solution)/shard_map/ppermute | solution.py:26
  57.4 66.3 %collective-permute-start.6 = (bf16[384,1792]{1,0:T(8,128)(2,1)S(1)}, bf16[384,1792]{1,0:T(8,128)(2,1)S(1)}, u32[]{:S(2)}, u32[]{:S(2)}) collective-permute-start(bf16[384,1792]{1,0:T(8,128)(2,1)S(1)} %bitcast.65), channel_id=1, source_target_pairs={{0,8},{8,0},{16,24},{24,16},{1,9},{9,1},{17,25},{25,17},{2,10},{10... | collective-permute-start | bytes 4128776 | tf_op jit(solution)/shard_map/ppermute | solution.py:26
  119.7 2.1 collective-permute-start.3
  119.8 32.8 %collective-permute-start.7 = (bf16[384,1792]{1,0:T(8,128)(2,1)}, bf16[384,1792]{1,0:T(8,128)(2,1)S(1)}, u32[]{:S(2)}, u32[]{:S(2)}) collective-permute-start(bf16[384,1792]{1,0:T(8,128)(2,1)} %bitcast.7), channel_id=1, source_target_pairs={{0,8},{8,0},{16,24},{24,16},{1,9},{9,1},{17,25},{25,17},{2,10},{10... | collective-permute-start | bytes 4128776 | tf_op jit(solution)/shard_map/ppermute | solution.py:26
  122.0 38.7 %collective-permute-start.4 = (bf16[384,768]{0,1:T(8,128)(2,1)S(1)}, bf16[384,768]{0,1:T(8,128)(2,1)S(1)}, u32[]{:S(2)}, u32[]{:S(2)}) collective-permute-start(bf16[384,768]{0,1:T(8,128)(2,1)S(1)} %add_convert_fusion.1), channel_id=1, source_target_pairs={{0,2},{1,3},{2,0},{3,1},{4,6},{5,7},{6,4},{7,5},{8,10},{9,11},{10,... | collective-permute-start | bytes 1769480 | tf_op jit(solution)/shard_map/ppermute | solution.py:26
  152.6 40.9 %copy-start.2 = (bf16[384,1792]{1,0:T(8,128)(2,1)}, bf16[384,1792]{1,0:T(8,128)(2,1)S(1)}, u32[]{:S(2)}) copy-start(bf16[384,1792]{1,0:T(8,128)(2,1)S(1)} %collective-permute-done.7) | copy-start | bytes 4128772
  160.6 2.1 collective-permute-start.8
  161.2 3.5 %collective-permute-start.5 = (bf16[384,768]{0,1:T(8,128)(2,1)S(1)}, bf16[384,768]{0,1:T(8,128)(2,1)S(1)}, u32[]{:S(2)}, u32[]{:S(2)}) collective-permute-start(bf16[384,768]{0,1:T(8,128)(2,1)S(1)} %pad_maximum_fusion.2), channel_id=1, source_target_pairs={{0,1},{1,0},{2,3},{3,2},{4,5},{5,4},{6,7},{7,6},{8,9},{9,8},{10,11... | collective-permute-start | bytes 1769480 | tf_op jit(solution)/shard_map/ppermute | solution.py:26
  162.9 15.4 %collective-permute-start.9 = (bf16[384,768]{0,1:T(8,128)(2,1)S(1)}, bf16[384,768]{0,1:T(8,128)(2,1)S(1)}, u32[]{:S(2)}, u32[]{:S(2)}) collective-permute-start(bf16[384,768]{0,1:T(8,128)(2,1)S(1)} %add_convert_fusion), channel_id=1, source_target_pairs={{0,2},{1,3},{2,0},{3,1},{4,6},{5,7},{6,4},{7,5},{8,10},{9,11},{10,... | collective-permute-start | bytes 1769480 | tf_op jit(solution)/shard_map/ppermute | solution.py:26
  164.9 58.0 %copy-start.4 = (bf16[384,768]{0,1:T(8,128)(2,1)}, bf16[384,768]{0,1:T(8,128)(2,1)S(1)}, u32[]{:S(2)}) copy-start(bf16[384,768]{0,1:T(8,128)(2,1)S(1)} %get-tuple-element.9) | copy-start | bytes 1769476
  178.8 3.6 %collective-permute-start.10 = (bf16[384,768]{0,1:T(8,128)(2,1)S(1)}, bf16[384,768]{0,1:T(8,128)(2,1)S(1)}, u32[]{:S(2)}, u32[]{:S(2)}) collective-permute-start(bf16[384,768]{0,1:T(8,128)(2,1)S(1)} %pad_maximum_fusion.5), channel_id=1, source_target_pairs={{0,1},{1,0},{2,3},{3,2},{4,5},{5,4},{6,7},{7,6},{8,9},{9,8},{10,11... | collective-permute-start | bytes 1769480 | tf_op jit(solution)/shard_map/ppermute | solution.py:26
  182.7 5.7 %copy-start.7 = (bf16[384,768]{0,1:T(8,128)(2,1)}, bf16[384,768]{0,1:T(8,128)(2,1)S(1)}, u32[]{:S(2)}) copy-start(bf16[384,768]{0,1:T(8,128)(2,1)S(1)} %get-tuple-element.4) | copy-start | bytes 1769476
  182.7 16.0 %copy-start.6 = (bf16[384,768]{0,1:T(8,128)(2,1)}, bf16[384,768]{0,1:T(8,128)(2,1)S(1)}, u32[]{:S(2)}) copy-start(bf16[384,768]{0,1:T(8,128)(2,1)S(1)} %get-tuple-element.5) | copy-start | bytes 1769476
  190.2 32.6 %collective-permute-start.11 = (bf16[384,1792]{1,0:T(8,128)(2,1)S(1)}, bf16[384,1792]{1,0:T(8,128)(2,1)S(1)}, u32[]{:S(2)}, u32[]{:S(2)}) collective-permute-start(bf16[384,1792]{1,0:T(8,128)(2,1)S(1)} %fusion.4), channel_id=1, source_target_pairs={{0,8},{8,0},{16,24},{24,16},{1,9},{9,1},{17,25},{25,17},{2,10},{10... | collective-permute-start | bytes 4128776 | tf_op jit(solution)/shard_map/ppermute | solution.py:26
  197.1 39.2 %collective-permute-start.14 = (bf16[256,1792]{1,0:T(8,128)(2,1)}, bf16[256,1792]{1,0:T(8,128)(2,1)}, u32[]{:S(2)}, u32[]{:S(2)}) collective-permute-start(bf16[256,1792]{1,0:T(8,128)(2,1)} %fusion.14), channel_id=1, source_target_pairs={{0,16},{8,24},{16,0},{24,8},{1,17},{9,25},{17,1},{25,9},{2,18},{10... | collective-permute-start | bytes 2752520 | tf_op jit(solution)/shard_map/ppermute | solution.py:26
  200.9 39.5 %collective-permute-start.13 = (bf16[256,1792]{1,0:T(8,128)(2,1)}, bf16[256,1792]{1,0:T(8,128)(2,1)}, u32[]{:S(2)}, u32[]{:S(2)}) collective-permute-start(bf16[256,1792]{1,0:T(8,128)(2,1)} %fusion.13), channel_id=1, source_target_pairs={{0,16},{8,24},{16,0},{24,8},{1,17},{9,25},{17,1},{25,9},{2,18},{10... | collective-permute-start | bytes 2752520 | tf_op jit(solution)/shard_map/ppermute | solution.py:26
  225.8 38.4 %all-to-all-start.2 = ((bf16[8,48,1792]{2,1,0:T(8,128)(2,1)}), bf16[8,48,1792]{2,1,0:T(8,128)(2,1)}, u32[]{:S(2)}, u32[]{:S(2)}) async-start(bf16[8,48,1792]{2,1,0:T(8,128)(2,1)} %bitcast.74), calls=%async_computation.2 | async-start | bytes 2752512 | tf_op jit(solution)/shard_map/all_to_all | solution.py:151
  232.1 2.3 copy-start.3
  232.1 2.3 copy-start.8
  232.8 26.3 %collective-permute-start.12 = (bf16[256,1792]{1,0:T(8,128)(2,1)S(1)}, bf16[256,1792]{1,0:T(8,128)(2,1)S(1)}, u32[]{:S(2)}, u32[]{:S(2)}) collective-permute-start(bf16[256,1792]{1,0:T(8,128)(2,1)S(1)} %fusion.12), channel_id=1, source_target_pairs={{0,16},{8,24},{16,0},{24,8},{1,17},{9,25},{17,1},{25,9},{2,18},{10... | collective-permute-start | bytes 2752520 | tf_op jit(solution)/shard_map/ppermute | solution.py:26
  235.7 1.1 copy-start.5
  266.5 2.0 copy-start.1

commit v2 on v1

--- a/solution.py
+++ b/solution.py
@@ -1,6 +1,8 @@
 import jax
 import jax.numpy as jnp
 from jax import lax
+from jax.experimental import pallas as pl
+from jax.experimental.pallas import tpu as pltpu
 from jax.sharding import PartitionSpec as P
 
 D = 7168
@@ -164,7 +166,313 @@
     return (in_grad, grad_gate, grad_up, grad_down)
 
 
+MESH = pl.DeviceIdType.MESH
+LANES = 256
+
+
+def flip(index, bit):
+    size = 1 << bit
+    return index + size - 2 * size * lax.rem(lax.div(index, size), 2)
+
+
+def expert_kernel(
+    xs, ds, wg, wu, wd, slot_rows, grad_gate, grad_up, grad_down,
+    x_all, d_all, w_all, give, keep, got, pair, across, act, act_t,
+    term_out, term_in, term_own, dx_out, dx_in, dx_own, dx_sum,
+    w_local, w_send, w_recv, self_sem, x_send, x_recv, d_send, d_recv,
+    fx_send, fx_recv, fd_send, fd_recv, give_send, give_recv, pair_send, pair_recv,
+    act_send, act_recv, term_send, term_recv, dx_send, dx_recv, back_send, back_recv,
+):
+    devices_ep, capacity, quarter = dx_sum.shape
+    rows = devices_ep * capacity
+    hidden = wg.shape[0]
+    r, s = lax.axis_index("dp"), lax.axis_index("ep")
+    core = lax.rem(s, 2)
+    row_mate, weight_mate = (flip(r, 0), s), (flip(r, 1), s)
+    core_mate, chip_mate = (r, flip(s, 0)), (r, flip(s, 1))
+    half = devices_ep // 2
+    order = sorted(range(1, devices_ep), key=lambda j: abs(j - half))
+
+    barrier = pltpu.get_barrier_semaphore()
+    peers = [row_mate, weight_mate]
+    peers += [(r, lax.rem(s + j, devices_ep)) for j in range(1, devices_ep)]
+    for peer in peers:
+        pl.semaphore_signal(barrier, inc=1, device_id=peer, device_id_type=MESH)
+    pl.semaphore_wait(barrier, len(peers))
+
+    def remote(source, target, send, recv, peer):
+        copy = pltpu.make_async_remote_copy(
+            src_ref=source, dst_ref=target, send_sem=send, recv_sem=recv,
+            device_id=peer, device_id_type=MESH,
+        )
+        copy.start()
+        return copy
+
+    def local(source, target, sem):
+        copy = pltpu.make_async_copy(source, target, sem)
+        copy.start()
+        return copy
+
+    def owned(ref, device):
+        row = pl.multiple_of(lax.div(device, GROUP) * capacity, capacity)
+        column = pl.multiple_of(lax.rem(device, GROUP) * quarter, 128)
+        return ref.at[pl.ds(row, capacity), pl.ds(column, quarter)]
+
+    sent = []
+    self_copies = [
+        local(owned(xs, s), x_all.at[0, s], self_sem.at[0]),
+        local(owned(ds, s), d_all.at[0, s], self_sem.at[1]),
+    ]
+    weights = (wg, wu, wd)
+    w_copies = [
+        remote(w, w_all.at[1, i], w_send.at[i], w_recv.at[i], weight_mate)
+        for i, w in enumerate(weights)
+    ]
+    own_w = [local(w, w_all.at[0, i], w_local.at[i]) for i, w in enumerate(weights)]
+    x_copies, d_copies = {}, {}
+    for copies, source, target, send, recv in (
+        (x_copies, xs, x_all, x_send, x_recv),
+        (d_copies, ds, d_all, d_send, d_recv),
+    ):
+        for j in order:
+            peer = lax.rem(s + j, devices_ep)
+            copies[j] = remote(
+                owned(source, peer), target.at[0, s], send.at[j], recv.at[j], (r, peer)
+            )
+    passed = []
+    for n, (copies, target, send, recv) in enumerate(
+        ((x_copies, x_all, fx_send, fx_recv), (d_copies, d_all, fd_send, fd_recv))
+    ):
+        self_copies[n].wait()
+        for j in [0] + order:
+            if j:
+                copies[j].wait_recv()
+            origin = lax.rem(s + devices_ep - j, devices_ep)
+            passed.append(
+                remote(
+                    target.at[0, origin], target.at[1, origin], send.at[j], recv.at[j], row_mate
+                )
+            )
+    for copy in own_w:
+        copy.wait()
+    for copy in w_copies:
+        copy.wait_recv()
+
+    def project(k, which, out):
+        for i in range(3):
+            block = (x_all if i < 2 else d_all)[k].reshape(rows, quarter)
+            out[k, :, i * hidden : (i + 1) * hidden] = dot_last(block, w_all[which, i]).astype(
+                jnp.bfloat16
+            )
+
+    STEP = 48
+
+    def by_rows(fn):
+        def one(n, carry):
+            fn(pl.ds(pl.multiple_of(n * STEP, STEP), STEP))
+            return carry
+
+        lax.fori_loop(0, rows // STEP, one, 0)
+
+    give_copies, pair_copies, act_copies = [], [], []
+    for k in range(2):
+        if k == 1:
+            for copy in passed:
+                copy.wait_recv()
+        project(k, 1 - core, give)
+        give_copies.append(
+            remote(give.at[k], got.at[k], give_send.at[k], give_recv.at[k], core_mate)
+        )
+        project(k, core, keep)
+        give_copies[k].wait_recv()
+
+        def add_pair(at, k=k):
+            pair[k, at, :] = (wide(keep[k, at, :]) + wide(got[k, at, :])).astype(jnp.bfloat16)
+
+        by_rows(add_pair)
+        pair_copies.append(
+            remote(pair.at[k], across.at[k], pair_send.at[k], pair_recv.at[k], chip_mate)
+        )
+    for k in range(2):
+        pair_copies[k].wait_recv()
+
+        def activate(at, k=k):
+            total = wide(pair[k, at, :]) + wide(across[k, at, :])
+            made = activations(
+                total[:, :hidden], total[:, hidden : 2 * hidden], total[:, 2 * hidden :]
+            )
+            for i in range(3):
+                act[k, core, at, i * hidden : (i + 1) * hidden] = made[i]
+
+        by_rows(activate)
+        act_copies.append(
+            remote(
+                act.at[k, core], act.at[k, core], act_send.at[k], act_recv.at[k], core_mate
+            )
+        )
+    for k in range(2):
+        act_copies[k].wait_recv()
+        for which in (1, 0):
+            act_t[which, :, k * rows : (k + 1) * rows] = act[k, which].T
+
+    def by_columns(fn):
+        def one(n, carry):
+            fn(pl.ds(pl.multiple_of(n * LANES, LANES), LANES))
+            return carry
+
+        lax.fori_loop(0, quarter // LANES, one, 0)
+
+    def term(which, i, at):
+        a = (i + 1) % 3 * hidden
+        block = (x_all if i < 2 else d_all)[:, :, :, at].reshape(2 * rows, LANES)
+        return jnp.dot(
+            act_t[which, a : a + hidden, :], block, preferred_element_type=jnp.float32
+        )
+
+    def expert_dx(k, at):
+        return sum(
+            jnp.dot(
+                act[k, which, :, (i + 1) * hidden : (i + 2) * hidden],
+                w_all[which, i, :, at],
+                preferred_element_type=jnp.float32,
+            )
+            for which in range(2)
+            for i in range(2)
+        ).reshape(devices_ep, capacity, LANES)
+
+    term_copies = []
+    for i in range(3):
+
+        def make_term(at, i=i):
+            term_out[i, :, at] = term(1, i, at).astype(jnp.bfloat16)
+
+        by_columns(make_term)
+        term_copies.append(
+            remote(
+                term_out.at[i], term_in.at[i], term_send.at[i], term_recv.at[i], weight_mate
+            )
+        )
+        if i == 0:
+
+            def make_dx(at):
+                dx_out[:, :, at] = expert_dx(1, at).astype(jnp.bfloat16)
+
+            by_columns(make_dx)
+            dx_copies = {}
+            for j in order + [0]:
+                block = lax.rem(s + j, devices_ep)
+                dx_copies[j] = remote(
+                    dx_out.at[block], dx_in.at[block], dx_send.at[j], dx_recv.at[j], row_mate
+                )
+
+    def own_dx(at):
+        dx_own[:, :, at] = expert_dx(0, at)
+
+    by_columns(own_dx)
+    for i in range(3):
+
+        def own_term(at, i=i):
+            term_own[i, :, at] = term(0, i, at)
+
+        by_columns(own_term)
+    backs = []
+    for j in order + [0]:
+        block = lax.rem(s + j, devices_ep)
+        dx_copies[j].wait_recv()
+        dx_sum[block] = (dx_own[block] + wide(dx_in[block])).astype(jnp.bfloat16)
+        if j:
+            backs.append(
+                remote(
+                    dx_sum.at[block], owned(slot_rows, s), back_send.at[j], back_recv.at[j],
+                    (r, block),
+                )
+            )
+        else:
+            last = local(dx_sum.at[block], owned(slot_rows, s), self_sem.at[2])
+    for i, out in enumerate((grad_gate, grad_up, grad_down)):
+        term_copies[i].wait_recv()
+
+        def finish(at, i=i, out=out):
+            out[:, at] = (term_own[i, :, at] + wide(term_in[i, :, at])).astype(jnp.bfloat16)
+
+        by_columns(finish)
+    last.wait()
+    for copy in backs:
+        copy.wait_recv()
+    sent = w_copies + list(x_copies.values()) + list(d_copies.values()) + passed
+    sent += give_copies + pair_copies + act_copies + term_copies + list(dx_copies.values())
+    for copy in sent + backs:
+        copy.wait_send()
+
+
+def fast_body(tokens, out_grad, route_weight, expert_ids, w_gate, w_up, w_down):
+    devices_ep = lax.axis_size("ep")
+    experts = devices_ep // GROUP
+    token_count = tokens.shape[0]
+    capacity = 6 * GROUP * token_count * TOP // (8 * devices_ep)
+    quarter = D // GROUP
+    hidden = w_gate.shape[0]
+    rows = devices_ep * capacity
+    short = jnp.bfloat16
+    _, _, token_of_slot, filled, weight_of_slot = slot_tables(
+        expert_ids, route_weight, experts, capacity
+    )
+    token_ids = jnp.arange(token_count, dtype=jnp.int32)
+    pick = ((token_of_slot[:, None] == token_ids[None, :]) & filled[:, None]).astype(short)
+    x_slots = jnp.dot(pick, tokens, preferred_element_type=jnp.float32).astype(short)
+    d_slots = (
+        jnp.dot(pick, out_grad, preferred_element_type=jnp.float32) * weight_of_slot[:, None]
+    ).astype(short)
+    vmem = pl.BlockSpec(memory_space=pltpu.VMEM)
+    hbm = pl.BlockSpec(memory_space=pl.ANY)
+    grad = jax.ShapeDtypeStruct(w_gate.shape, short)
+    dma = pltpu.SemaphoreType.DMA
+    slot_rows, grad_gate, grad_up, grad_down = pl.pallas_call(
+        expert_kernel,
+        out_shape=(jax.ShapeDtypeStruct(x_slots.shape, short), grad, grad, grad),
+        in_specs=[vmem, vmem, hbm, hbm, hbm],
+        out_specs=(vmem, vmem, vmem, vmem),
+        scratch_shapes=[
+            pltpu.VMEM((2, devices_ep, capacity, quarter), short),
+            pltpu.VMEM((2, devices_ep, capacity, quarter), short),
+            pltpu.VMEM((2, 3, hidden, quarter), short),
+            pltpu.VMEM((2, rows, 3 * hidden), short),
+            pltpu.VMEM((2, rows, 3 * hidden), short),
+            pltpu.VMEM((2, rows, 3 * hidden), short),
+            pltpu.VMEM((2, rows, 3 * hidden), short),
+            pltpu.VMEM((2, rows, 3 * hidden), short),
+            pltpu.VMEM((2, 2, rows, 3 * hidden), short),
+            pltpu.VMEM((2, 3 * hidden, 2 * rows), short),
+            pltpu.VMEM((3, hidden, quarter), short),
+            pltpu.VMEM((3, hidden, quarter), short),
+            pltpu.VMEM((3, hidden, quarter), jnp.float32),
+            pltpu.VMEM((devices_ep, capacity, quarter), short),
+            pltpu.VMEM((devices_ep, capacity, quarter), short),
+            pltpu.VMEM((devices_ep, capacity, quarter), jnp.float32),
+            pltpu.VMEM((devices_ep, capacity, quarter), short),
+        ]
+        + [dma((3,))] * 4
+        + [dma((devices_ep,))] * 8
+        + [dma((2,))] * 6
+        + [dma((3,))] * 2
+        + [dma((devices_ep,))] * 4,
+        compiler_params=pltpu.CompilerParams(
+            collective_id=0, has_side_effects=True, vmem_limit_bytes=60 * 2**20
+        ),
+    )(x_slots, d_slots, w_gate, w_up, w_down)
+    in_grad = dot_first(pick, slot_rows).astype(short)
+    return (in_grad, grad_gate, grad_up, grad_down)
+
+
 def solution(mesh):
+    devices_ep = mesh.shape["ep"]
+
+    def step(*arrays):
+        capacity = 6 * GROUP * arrays[0].shape[0] * TOP // (8 * devices_ep)
+        hidden = arrays[4].shape[0]
+        fits = capacity % 48 == 0 and hidden % 128 == 0 and mesh.shape["dp"] == 4
+        return (fast_body if fits else body)(*arrays)
+
     placed = (
         P(("dp", "ep"), None),
         P(("dp", "ep"), None),
@@ -175,7 +483,7 @@
         P("dp", "ep"),
     )
     return jax.shard_map(
-        body,
+        step,
         mesh=mesh,
         in_specs=placed,
         out_specs=(P(("dp", "ep"), None), P("dp", "ep"), P("dp", "ep"), P("dp", "ep")),

time: 270 us -> 195 us (0.72)
  Pallas kernels: 0 us -> 181 us
  waiting for transfers between devices: 157 us -> 0 us
  matrix products: 62.3 us -> 6.77 us
  starting transfers between devices: 31.7 us -> 0 us
  local copies, waits for them, and re-layouts: 11.3 us -> 2.79 us
    pallas_call x0 -> x1, Pallas kernels: none -> 181 us  [fast_body(): pl.pallas_call(expert_kernel, out_shape=(jax.ShapeDtypeStruct(x_slots.sha...]
    ppermute x15 -> x0, waiting for transfers between devices: 102 us -> none  [from_partner(): return lax.ppermute(value, axis, pairs)]
    all_to_all x3 -> x0, waiting for transfers between devices: 55.1 us -> none  [the longest x2 51.5 us: sent(): lax.all_to_all(to_owners(rows), 'ep', split_axis=0, concat_axis=0, tiled=...]
    dot_general x22 -> x2, matrix products: 42.8 us -> 3.31 us  [the longest x1 1.66 us: fast_body(): jnp.dot(pick, out_grad, preferred_element_type=jnp.float32)]
    ppermute x15 -> x0, starting transfers between devices: 16 us -> none  [from_partner(): return lax.ppermute(value, axis, pairs)]
    dot_general x13 -> x1, matrix products: 19.5 us -> 3.46 us  [dot_first(): lax.dot_general(left, right, CONTRACT_FIRST, preferred_element_type=jnp.f...]
    all_to_all x3 -> x0, starting transfers between devices: 15.7 us -> none  [the longest x2 10.9 us: sent(): lax.all_to_all(to_owners(rows), 'ep', split_axis=0, concat_axis=0, tiled=...]
    reshape x4 -> x0, local copies, waits for them, and re-layouts: 8.64 us -> none  [to_owners(): rows.reshape(experts, capacity, GROUP, quarter).transpose(0, 2, 1, 3)]
  transfers between devices with their start and end apart: 18 -> 0, of which waited for: 11 -> 0; matrix products, arithmetic and copies ran while one was open for 21% -> 0% of each run, Pallas kernels for 0% -> 0%
where the time goes in v2:
time: 195 us
  Pallas kernels  181 us (93%)
  matrix products  6.77 us (3%)
  other arithmetic  3.67 us (2%)
  local copies, waits for them, and re-layouts  2.79 us (1%)
    pallas_call x1, Pallas kernels, fast_body(): pl.pallas_call(expert_kernel, out_shape=(jax.ShapeDtypeStruct(x_slots.sha...  181 us

profile of v2, /device:TPU:0, one launch (start us, length us, event | category | flops | bytes accessed | tf_op | source)
XLA Modules:
  0.0 194.7 jit_solution(476147302187261029)
XLA Ops:
  0.6 0.0 copy-start
  0.6 0.9 fusion.1
  1.5 0.2 reduce_window_sum.11
  1.7 0.0 copy-start.1
  1.7 1.0 select_reduce_fusion
  2.7 0.7 add_select_fusion
  3.3 0.1 fusion.3
  3.5 0.1 select_reduce_fusion.2
  3.6 0.8 select_reduce_fusion.1
  4.4 0.0 copy-done
  4.4 1.7 fusion.ds
  6.0 0.0 copy-done.1
  6.0 1.7 convolution_convert_fusion.1.xs
  7.7 180.7 %shard_map.102 = (bf16[96,7168]{1,0:T(8,128)(2,1)}, bf16[256,1792]{1,0:T(8,128)(2,1)}, bf16[256,1792]{1,0:T(8,128)(2,1)}, bf16[256,1792]{1,0:T(8,128)(2,1)}) custom-call(bf16[96,7168]{1,0:T(8,128)(2,1)} %convolution_convert_fusion.1.xs, bf16[96,7168]{1,0:T(8,128)(2,1)} %fusion.ds, bf16[256,1792]{1,0:T(8,128)(2,1)} %wg.1, bf16[256,1792]{1,0:T(8,128)(2,1)} %wu.1, ...), custom_call_target="tpu_custom_call" | custom-call | tf_op jit(solution)/shard_map/pallas_call | solution.py:430
  188.4 0.0 copy-start.4
  188.4 0.0 copy-start.3
  188.4 3.5 %convolution_convert_fusion = bf16[128,7168]{1,0:T(8,128)(2,1)} fusion(bf16[96,7168]{1,0:T(8,128)(2,1)} %get-tuple-element.8, s32[96]{0:T(128)S(1)} %select_reduce_fusion.2, pred[96]{0:T(512)(128)(4,1)S(1)} %fusion.3), kind=kOutput, calls=%fused_computation | convolution fusion | flops 177102848 | bytes 3211744 | tf_op jit(solution)/shard_map/dot_general | solution.py:72
  191.9 0.0 copy-done.4
  191.9 0.0 copy-start.2
  191.9 0.9 copy.14
  192.8 0.0 copy-done.3
  192.8 0.9 copy.15
  193.7 0.0 copy-done.2
  193.7 0.9 copy.16
  (1 shorter events, 0.0 us)
Async XLA Ops:
  0.6 3.7 %copy-start = (bf16[128,7168]{1,0:T(8,128)(2,1)S(1)}, bf16[128,7168]{1,0:T(8,128)(2,1)}, u32[]{:S(2)}) copy-start(bf16[128,7168]{1,0:T(8,128)(2,1)} %param.8) | copy-start | bytes 5505028
  1.7 4.3 %copy-start.1 = (bf16[128,7168]{1,0:T(8,128)(2,1)S(1)}, bf16[128,7168]{1,0:T(8,128)(2,1)}, u32[]{:S(2)}) copy-start(bf16[128,7168]{1,0:T(8,128)(2,1)} %param.7) | copy-start | bytes 5505028
  188.4 3.5 %copy-start.4 = (bf16[256,1792]{1,0:T(8,128)(2,1)S(1)}, bf16[256,1792]{1,0:T(8,128)(2,1)}, u32[]{:S(2)}) copy-start(bf16[256,1792]{1,0:T(8,128)(2,1)} %get-tuple-element.17) | copy-start | bytes 2752516
  188.4 4.4 %copy-start.3 = (bf16[256,1792]{1,0:T(8,128)(2,1)S(1)}, bf16[256,1792]{1,0:T(8,128)(2,1)}, u32[]{:S(2)}) copy-start(bf16[256,1792]{1,0:T(8,128)(2,1)} %get-tuple-element.18) | copy-start | bytes 2752516
  191.9 1.9 copy-start.2

commit v3 on v2

--- a/solution.py
+++ b/solution.py
@@ -176,8 +176,8 @@
 
 
 def expert_kernel(
-    xs, ds, wg, wu, wd, slot_rows, grad_gate, grad_up, grad_down,
-    x_all, d_all, w_all, give, keep, got, pair, across, act, act_t,
+    tokens, out_grad, pick, pick_t, scale, wg, wu, wd, in_grad, grad_gate, grad_up, grad_down,
+    xs, ds, slot_rows, x_all, d_all, w_all, part, got, pair, across, act, act_t,
     term_out, term_in, term_own, dx_out, dx_in, dx_own, dx_sum,
     w_local, w_send, w_recv, self_sem, x_send, x_recv, d_send, d_recv,
     fx_send, fx_recv, fd_send, fd_recv, give_send, give_recv, pair_send, pair_recv,
@@ -218,11 +218,25 @@
         column = pl.multiple_of(lax.rem(device, GROUP) * quarter, 128)
         return ref.at[pl.ds(row, capacity), pl.ds(column, quarter)]
 
-    sent = []
-    self_copies = [
-        local(owned(xs, s), x_all.at[0, s], self_sem.at[0]),
-        local(owned(ds, s), d_all.at[0, s], self_sem.at[1]),
-    ]
+    WIDE = 4 * 128
+
+    def by_slots(fn):
+        def one(n, carry):
+            fn(pl.ds(pl.multiple_of(n * WIDE, WIDE), WIDE))
+            return carry
+
+        lax.fori_loop(0, xs.shape[1] // WIDE, one, 0)
+
+    def fill_x(at):
+        xs[:, at] = jnp.dot(
+            pick[...], tokens[:, at], preferred_element_type=jnp.float32
+        ).astype(jnp.bfloat16)
+
+    def fill_d(at):
+        ds[:, at] = (
+            jnp.dot(pick[...], out_grad[:, at], preferred_element_type=jnp.float32) * scale[...]
+        ).astype(jnp.bfloat16)
+
     weights = (wg, wu, wd)
     w_copies = [
         remote(w, w_all.at[1, i], w_send.at[i], w_recv.at[i], weight_mate)
@@ -230,40 +244,38 @@
     ]
     own_w = [local(w, w_all.at[0, i], w_local.at[i]) for i, w in enumerate(weights)]
     x_copies, d_copies = {}, {}
-    for copies, source, target, send, recv in (
-        (x_copies, xs, x_all, x_send, x_recv),
-        (d_copies, ds, d_all, d_send, d_recv),
-    ):
+    self_copies = []
+    for n, (fill, copies, source, target, send, recv) in enumerate((
+        (fill_x, x_copies, xs, x_all, x_send, x_recv),
+        (fill_d, d_copies, ds, d_all, d_send, d_recv),
+    )):
+        by_slots(fill)
         for j in order:
             peer = lax.rem(s + j, devices_ep)
             copies[j] = remote(
                 owned(source, peer), target.at[0, s], send.at[j], recv.at[j], (r, peer)
             )
-    passed = []
-    for n, (copies, target, send, recv) in enumerate(
-        ((x_copies, x_all, fx_send, fx_recv), (d_copies, d_all, fd_send, fd_recv))
-    ):
-        self_copies[n].wait()
-        for j in [0] + order:
-            if j:
-                copies[j].wait_recv()
-            origin = lax.rem(s + devices_ep - j, devices_ep)
-            passed.append(
-                remote(
-                    target.at[0, origin], target.at[1, origin], send.at[j], recv.at[j], row_mate
-                )
-            )
-    for copy in own_w:
-        copy.wait()
-    for copy in w_copies:
-        copy.wait_recv()
-
-    def project(k, which, out):
-        for i in range(3):
+        self_copies.append(local(owned(source, s), target.at[0, s], self_sem.at[n]))
+    passed = ([], [])
+
+    def pass_on(n, j):
+        copies, target, send, recv = (
+            (x_copies, x_all, fx_send, fx_recv),
+            (d_copies, d_all, fd_send, fd_recv),
+        )[n]
+        if j:
+            copies[j].wait_recv()
+        else:
+            self_copies[n].wait()
+        origin = lax.rem(s + devices_ep - j, devices_ep)
+        passed[n].append(
+            remote(target.at[0, origin], target.at[1, origin], send.at[j], recv.at[j], row_mate)
+        )
+
+    def project(k, which, pieces):
+        for i in pieces:
             block = (x_all if i < 2 else d_all)[k].reshape(rows, quarter)
-            out[k, :, i * hidden : (i + 1) * hidden] = dot_last(block, w_all[which, i]).astype(
-                jnp.bfloat16
-            )
+            part[k, which, i] = dot_last(block, w_all[which, i]).astype(jnp.bfloat16)
 
     STEP = 48
 
@@ -274,33 +286,79 @@
 
         lax.fori_loop(0, rows // STEP, one, 0)
 
-    give_copies, pair_copies, act_copies = [], [], []
+    give_copies, pair_copies, act_copies = {}, {}, []
+    groups = ((0, 1), (2,))
+
+    def hand_over(k, g):
+        pieces = pl.ds(groups[g][0], len(groups[g]))
+        give_copies[k, g] = remote(
+            part.at[k, 1 - core, pieces], got.at[k, pieces],
+            give_send.at[2 * k + g], give_recv.at[2 * k + g], core_mate,
+        )
+
+    def send_pair(k, g):
+        give_copies[k, g].wait_recv()
+
+        def add_pair(at):
+            for i in groups[g]:
+                pair[k, i, at, :] = (wide(part[k, core, i, at, :]) + wide(got[k, i, at, :])).astype(
+                    jnp.bfloat16
+                )
+
+        by_rows(add_pair)
+        pieces = pl.ds(groups[g][0], len(groups[g]))
+        pair_copies[k, g] = remote(
+            pair.at[k, pieces], across.at[k, pieces],
+            pair_send.at[2 * k + g], pair_recv.at[2 * k + g], chip_mate,
+        )
+
+    def gate_up_first():
+        project(0, 0, (0, 1))
+
+    def gate_up_second():
+        for i in range(2):
+            w_copies[i].wait_recv()
+        project(0, 1, (0, 1))
+        hand_over(0, 0)
+
+    def gate_up_third():
+        for copy in passed[0]:
+            copy.wait_recv()
+        project(1, 0, (0, 1))
+
+    def gate_up_fourth():
+        send_pair(0, 0)
+        project(1, 1, (0, 1))
+        hand_over(1, 0)
+
+    between = {3: gate_up_first, 4: gate_up_second, 5: gate_up_third, 6: gate_up_fourth}
+    for j in [0] + order:
+        pass_on(0, j)
+    for copy in own_w:
+        copy.wait()
+    for n, j in enumerate([0] + order):
+        pass_on(1, j)
+        if n in between:
+            between[n]()
+    send_pair(1, 0)
+    w_copies[2].wait_recv()
+    for which in range(2):
+        project(0, which, (2,))
+    hand_over(0, 1)
+    for copy in passed[1]:
+        copy.wait_recv()
+    for which in range(2):
+        project(1, which, (2,))
+    hand_over(1, 1)
     for k in range(2):
-        if k == 1:
-            for copy in passed:
-                copy.wait_recv()
-        project(k, 1 - core, give)
-        give_copies.append(
-            remote(give.at[k], got.at[k], give_send.at[k], give_recv.at[k], core_mate)
-        )
-        project(k, core, keep)
-        give_copies[k].wait_recv()
-
-        def add_pair(at, k=k):
-            pair[k, at, :] = (wide(keep[k, at, :]) + wide(got[k, at, :])).astype(jnp.bfloat16)
-
-        by_rows(add_pair)
-        pair_copies.append(
-            remote(pair.at[k], across.at[k], pair_send.at[k], pair_recv.at[k], chip_mate)
-        )
+        send_pair(k, 1)
     for k in range(2):
-        pair_copies[k].wait_recv()
+        for g in range(2):
+            pair_copies[k, g].wait_recv()
 
         def activate(at, k=k):
-            total = wide(pair[k, at, :]) + wide(across[k, at, :])
-            made = activations(
-                total[:, :hidden], total[:, hidden : 2 * hidden], total[:, 2 * hidden :]
-            )
+            total = [wide(pair[k, i, at, :]) + wide(across[k, i, at, :]) for i in range(3)]
+            made = activations(*total)
             for i in range(3):
                 act[k, core, at, i * hidden : (i + 1) * hidden] = made[i]
 
@@ -310,10 +368,14 @@
                 act.at[k, core], act.at[k, core], act_send.at[k], act_recv.at[k], core_mate
             )
         )
+
+    def transpose(which):
+        for k in range(2):
+            act_t[which, :, k * rows : (k + 1) * rows] = act[k, which].T
+
     for k in range(2):
         act_copies[k].wait_recv()
-        for which in (1, 0):
-            act_t[which, :, k * rows : (k + 1) * rows] = act[k, which].T
+    transpose(1)
 
     def by_columns(fn):
         def one(n, carry):
@@ -369,6 +431,7 @@
         dx_own[:, :, at] = expert_dx(0, at)
 
     by_columns(own_dx)
+    transpose(0)
     for i in range(3):
 
         def own_term(at, i=i):
@@ -389,18 +452,25 @@
             )
         else:
             last = local(dx_sum.at[block], owned(slot_rows, s), self_sem.at[2])
-    for i, out in enumerate((grad_gate, grad_up, grad_down)):
-        term_copies[i].wait_recv()
-
-        def finish(at, i=i, out=out):
-            out[:, at] = (term_own[i, :, at] + wide(term_in[i, :, at])).astype(jnp.bfloat16)
-
-        by_columns(finish)
     last.wait()
     for copy in backs:
         copy.wait_recv()
-    sent = w_copies + list(x_copies.values()) + list(d_copies.values()) + passed
-    sent += give_copies + pair_copies + act_copies + term_copies + list(dx_copies.values())
+
+    def fill_in(at):
+        in_grad[:, at] = jnp.dot(
+            pick_t[...], slot_rows[:, at], preferred_element_type=jnp.float32
+        ).astype(jnp.bfloat16)
+
+    by_slots(fill_in)
+    for i, out in enumerate((grad_gate, grad_up, grad_down)):
+        term_copies[i].wait_recv()
+
+        def finish(at, i=i, out=out):
+            out[:, at] = (term_own[i, :, at] + wide(term_in[i, :, at])).astype(jnp.bfloat16)
+
+        by_columns(finish)
+    sent = w_copies + list(x_copies.values()) + list(d_copies.values()) + passed[0] + passed[1]
+    sent += list(give_copies.values()) + list(pair_copies.values()) + act_copies + term_copies + list(dx_copies.values())
     for copy in sent + backs:
         copy.wait_send()
 
@@ -419,28 +489,27 @@
     )
     token_ids = jnp.arange(token_count, dtype=jnp.int32)
     pick = ((token_of_slot[:, None] == token_ids[None, :]) & filled[:, None]).astype(short)
-    x_slots = jnp.dot(pick, tokens, preferred_element_type=jnp.float32).astype(short)
-    d_slots = (
-        jnp.dot(pick, out_grad, preferred_element_type=jnp.float32) * weight_of_slot[:, None]
-    ).astype(short)
+    pick_t = ((token_of_slot[None, :] == token_ids[:, None]) & filled[None, :]).astype(short)
     vmem = pl.BlockSpec(memory_space=pltpu.VMEM)
     hbm = pl.BlockSpec(memory_space=pl.ANY)
     grad = jax.ShapeDtypeStruct(w_gate.shape, short)
     dma = pltpu.SemaphoreType.DMA
-    slot_rows, grad_gate, grad_up, grad_down = pl.pallas_call(
+    in_grad, grad_gate, grad_up, grad_down = pl.pallas_call(
         expert_kernel,
-        out_shape=(jax.ShapeDtypeStruct(x_slots.shape, short), grad, grad, grad),
-        in_specs=[vmem, vmem, hbm, hbm, hbm],
+        out_shape=(jax.ShapeDtypeStruct(tokens.shape, short), grad, grad, grad),
+        in_specs=[vmem, vmem, vmem, vmem, vmem, hbm, hbm, hbm],
         out_specs=(vmem, vmem, vmem, vmem),
         scratch_shapes=[
+            pltpu.VMEM((experts * capacity, D), short),
+            pltpu.VMEM((experts * capacity, D), short),
+            pltpu.VMEM((experts * capacity, D), short),
             pltpu.VMEM((2, devices_ep, capacity, quarter), short),
             pltpu.VMEM((2, devices_ep, capacity, quarter), short),
             pltpu.VMEM((2, 3, hidden, quarter), short),
-            pltpu.VMEM((2, rows, 3 * hidden), short),
-            pltpu.VMEM((2, rows, 3 * hidden), short),
-            pltpu.VMEM((2, rows, 3 * hidden), short),
-            pltpu.VMEM((2, rows, 3 * hidden), short),
-            pltpu.VMEM((2, rows, 3 * hidden), short),
+            pltpu.VMEM((2, 2, 3, rows, hidden), short),
+            pltpu.VMEM((2, 3, rows, hidden), short),
+            pltpu.VMEM((2, 3, rows, hidden), short),
+            pltpu.VMEM((2, 3, rows, hidden), short),
             pltpu.VMEM((2, 2, rows, 3 * hidden), short),
             pltpu.VMEM((2, 3 * hidden, 2 * rows), short),
             pltpu.VMEM((3, hidden, quarter), short),
@@ -453,14 +522,14 @@
         ]
         + [dma((3,))] * 4
         + [dma((devices_ep,))] * 8
-        + [dma((2,))] * 6
+        + [dma((4,))] * 4
+        + [dma((2,))] * 2
         + [dma((3,))] * 2
         + [dma((devices_ep,))] * 4,
         compiler_params=pltpu.CompilerParams(
             collective_id=0, has_side_effects=True, vmem_limit_bytes=60 * 2**20
         ),
-    )(x_slots, d_slots, w_gate, w_up, w_down)
-    in_grad = dot_first(pick, slot_rows).astype(short)
+    )(tokens, out_grad, pick, pick_t, weight_of_slot[:, None], w_gate, w_up, w_down)
     return (in_grad, grad_gate, grad_up, grad_down)
 
 

time: 195 us -> 189 us (0.969)
  matrix products: 6.77 us -> 0 us
  Pallas kernels: 181 us -> 176 us
  local copies, waits for them, and re-layouts: 2.79 us -> 7.01 us
    dot_general x3 -> x0, matrix products: 6.77 us -> none  [the longest x1 3.46 us: dot_first(): lax.dot_general(left, right, CONTRACT_FIRST, preferred_element_type=jnp.f...]
    pallas_call x1, Pallas kernels: 181 us -> 176 us  [fast_body(): pl.pallas_call(expert_kernel, out_shape=(jax.ShapeDtypeStruct(tokens.shap...]
    unnamed x13 -> x10, local copies, waits for them, and re-layouts: 2.79 us -> 6.29 us
where the time goes in v3:
time: 189 us; the launch traced here: 188 us
  Pallas kernels  176 us (93%)
  local copies, waits for them, and re-layouts  7.01 us (4%)
  other arithmetic  4.75 us (3%)
    pallas_call x1, Pallas kernels, fast_body(): pl.pallas_call(expert_kernel, out_shape=(jax.ShapeDtypeStruct(tokens.shap...  176 us
    unnamed x10, local copies, waits for them, and re-layouts  6.29 us

profile of v3, /device:TPU:0, one launch (start us, length us, event | category | flops | bytes accessed | tf_op | source)
XLA Modules:
  0.0 188.4 jit_solution(7477746050032154946)
XLA Ops:
  0.6 0.7 fusion
  1.4 0.2 reduce_window_sum.11
  1.5 0.8 select_reduce_fusion
  2.4 0.7 add_select_fusion
  3.1 0.1 fusion.4
  3.2 0.1 select_reduce_fusion.2
  3.3 0.8 select_reduce_fusion.1
  4.1 0.7 fusion.6.pick
  4.8 0.6 fusion.2.pick_t
  5.4 0.7 copy.12.scale
  6.1 175.9 %shard_map.102 = (bf16[128,7168]{1,0:T(8,128)(2,1)}, bf16[256,1792]{1,0:T(8,128)(2,1)}, bf16[256,1792]{1,0:T(8,128)(2,1)}, bf16[256,1792]{1,0:T(8,128)(2,1)}) custom-call(bf16[128,7168]{1,0:T(8,128)(2,1)} %tokens.1, bf16[128,7168]{1,0:T(8,128)(2,1)} %out_grad.1, bf16[96,128]{1,0:T(8,128)(2,1)} %fusion.6.pick, bf16[128,96]{1,0:T(8,128)(2,1)} %fusion.2.pick_t, ...), custom_call_target="tpu_custom_call" | custom-call | tf_op jit(solution)/shard_map/pallas_call | solution.py:497
  182.1 0.0 copy-start.2
  182.1 2.9 %copy.17 = bf16[128,7168]{1,0:T(8,128)(2,1)} copy(bf16[128,7168]{1,0:T(8,128)(2,1)} %get-tuple-element.8) | data formatting | bytes 3670016
  185.0 0.0 copy-done.2
  185.0 0.0 copy-start.1
  185.0 0.0 copy-start
  185.0 0.9 copy.18
  186.0 0.6 copy-done.1
  186.5 0.9 copy.19
  187.5 0.0 copy-done
  187.5 0.9 copy.20
  (1 shorter events, 0.0 us)
Async XLA Ops:
  182.1 2.9 %copy-start.2 = (bf16[256,1792]{1,0:T(8,128)(2,1)S(1)}, bf16[256,1792]{1,0:T(8,128)(2,1)}, u32[]{:S(2)}) copy-start(bf16[256,1792]{1,0:T(8,128)(2,1)} %get-tuple-element.9) | copy-start | bytes 2752516
  185.0 1.5 copy-start.1
  185.0 2.4 %copy-start = (bf16[256,1792]{1,0:T(8,128)(2,1)S(1)}, bf16[256,1792]{1,0:T(8,128)(2,1)}, u32[]{:S(2)}) copy-start(bf16[256,1792]{1,0:T(8,128)(2,1)} %get-tuple-element.11) | copy-start | bytes 2752516

commit v4 on v3

--- a/solution.py
+++ b/solution.py
@@ -190,12 +190,18 @@
     core = lax.rem(s, 2)
     row_mate, weight_mate = (flip(r, 0), s), (flip(r, 1), s)
     core_mate, chip_mate = (r, flip(s, 0)), (r, flip(s, 1))
-    half = devices_ep // 2
-    order = sorted(range(1, devices_ep), key=lambda j: abs(j - half))
+    order = list(range(devices_ep - 1, 0, -1))
+
+    def mate(mask):
+        index = s
+        for bit in range(mask.bit_length()):
+            if mask >> bit & 1:
+                index = flip(index, bit)
+        return index
 
     barrier = pltpu.get_barrier_semaphore()
     peers = [row_mate, weight_mate]
-    peers += [(r, lax.rem(s + j, devices_ep)) for j in range(1, devices_ep)]
+    peers += [(r, mate(j)) for j in range(1, devices_ep)]
     for peer in peers:
         pl.semaphore_signal(barrier, inc=1, device_id=peer, device_id_type=MESH)
     pl.semaphore_wait(barrier, len(peers))
@@ -251,7 +257,7 @@
     )):
         by_slots(fill)
         for j in order:
-            peer = lax.rem(s + j, devices_ep)
+            peer = mate(j)
             copies[j] = remote(
                 owned(source, peer), target.at[0, s], send.at[j], recv.at[j], (r, peer)
             )
@@ -267,7 +273,7 @@
             copies[j].wait_recv()
         else:
             self_copies[n].wait()
-        origin = lax.rem(s + devices_ep - j, devices_ep)
+        origin = mate(j)
         passed[n].append(
             remote(target.at[0, origin], target.at[1, origin], send.at[j], recv.at[j], row_mate)
         )
@@ -331,15 +337,23 @@
         project(1, 1, (0, 1))
         hand_over(1, 0)
 
-    between = {3: gate_up_first, 4: gate_up_second, 5: gate_up_third, 6: gate_up_fourth}
-    for j in [0] + order:
-        pass_on(0, j)
+    near, far = list(range(GROUP)), list(range(GROUP, devices_ep))[::-1]
+    arrivals = [(0, j) for j in near]
+    for n, j in enumerate(far):
+        arrivals.append((0, j))
+        if 0 < n <= GROUP:
+            arrivals.append((1, near[n - 1]))
+    arrivals += [(1, j) for j in near if (1, j) not in arrivals]
+    for n, j in arrivals:
+        pass_on(n, j)
     for copy in own_w:
         copy.wait()
-    for n, j in enumerate([0] + order):
+    gate_up_first()
+    steps = [gate_up_second, gate_up_third, gate_up_fourth]
+    for n, j in enumerate(far):
         pass_on(1, j)
-        if n in between:
-            between[n]()
+        if n < len(steps):
+            steps[n]()
     send_pair(1, 0)
     w_copies[2].wait_recv()
     for which in range(2):
@@ -422,7 +436,7 @@
             by_columns(make_dx)
             dx_copies = {}
             for j in order + [0]:
-                block = lax.rem(s + j, devices_ep)
+                block = mate(j)
                 dx_copies[j] = remote(
                     dx_out.at[block], dx_in.at[block], dx_send.at[j], dx_recv.at[j], row_mate
                 )
@@ -440,7 +454,7 @@
         by_columns(own_term)
     backs = []
     for j in order + [0]:
-        block = lax.rem(s + j, devices_ep)
+        block = mate(j)
         dx_copies[j].wait_recv()
         dx_sum[block] = (dx_own[block] + wide(dx_in[block])).astype(jnp.bfloat16)
         if j:
@@ -452,17 +466,21 @@
             )
         else:
             last = local(dx_sum.at[block], owned(slot_rows, s), self_sem.at[2])
-    last.wait()
-    for copy in backs:
-        copy.wait_recv()
-
-    def fill_in(at):
-        in_grad[:, at] = jnp.dot(
-            pick_t[...], slot_rows[:, at], preferred_element_type=jnp.float32
-        ).astype(jnp.bfloat16)
-
-    by_slots(fill_in)
+    def take_back():
+        last.wait()
+        for copy in backs:
+            copy.wait_recv()
+
+        def fill_in(at):
+            in_grad[:, at] = jnp.dot(
+                pick_t[...], slot_rows[:, at], preferred_element_type=jnp.float32
+            ).astype(jnp.bfloat16)
+
+        by_slots(fill_in)
+
     for i, out in enumerate((grad_gate, grad_up, grad_down)):
+        if i == 2:
+            take_back()
         term_copies[i].wait_recv()
 
         def finish(at, i=i, out=out):

time: 189 us -> 178 us (0.942)
  Pallas kernels: 176 us -> 164 us
    pallas_call x1, Pallas kernels: 176 us -> 164 us  [fast_body(): pl.pallas_call(expert_kernel, out_shape=(jax.ShapeDtypeStruct(tokens.shap...]
where the time goes in v4:
time: 178 us; the launch traced here: 177 us
  Pallas kernels  164 us (92%)
  local copies, waits for them, and re-layouts  7.01 us (4%)
  other arithmetic  4.75 us (3%)
    pallas_call x1, Pallas kernels, fast_body(): pl.pallas_call(expert_kernel, out_shape=(jax.ShapeDtypeStruct(tokens.shap...  164 us
    unnamed x10, local copies, waits for them, and re-layouts  6.29 us

profile of v4, /device:TPU:0, one launch (start us, length us, event | category | flops | bytes accessed | tf_op | source)
XLA Modules:
  0.0 176.8 jit_solution(17567336184879362536)
XLA Ops:
  0.6 0.7 fusion
  1.4 0.2 reduce_window_sum.11
  1.5 0.8 select_reduce_fusion
  2.4 0.7 add_select_fusion
  3.1 0.1 fusion.4
  3.2 0.1 select_reduce_fusion.2
  3.3 0.8 select_reduce_fusion.1
  4.1 0.7 fusion.6.pick
  4.8 0.6 fusion.2.pick_t
  5.4 0.7 copy.12.scale
  6.1 164.4 %shard_map.102 = (bf16[128,7168]{1,0:T(8,128)(2,1)}, bf16[256,1792]{1,0:T(8,128)(2,1)}, bf16[256,1792]{1,0:T(8,128)(2,1)}, bf16[256,1792]{1,0:T(8,128)(2,1)}) custom-call(bf16[128,7168]{1,0:T(8,128)(2,1)} %tokens.1, bf16[128,7168]{1,0:T(8,128)(2,1)} %out_grad.1, bf16[96,128]{1,0:T(8,128)(2,1)} %fusion.6.pick, bf16[128,96]{1,0:T(8,128)(2,1)} %fusion.2.pick_t, ...), custom_call_target="tpu_custom_call" | custom-call | tf_op jit(solution)/shard_map/pallas_call | solution.py:515
  170.5 0.0 copy-start.2
  170.5 2.9 %copy.17 = bf16[128,7168]{1,0:T(8,128)(2,1)} copy(bf16[128,7168]{1,0:T(8,128)(2,1)} %get-tuple-element.8) | data formatting | bytes 3670016
  173.4 0.0 copy-done.2
  173.4 0.0 copy-start.1
  173.4 0.0 copy-start
  173.5 0.9 copy.18
  174.4 0.6 copy-done.1
  175.0 0.9 copy.19
  175.9 0.0 copy-done
  175.9 0.9 copy.20
  (1 shorter events, 0.0 us)
Async XLA Ops:
  170.5 2.9 %copy-start.2 = (bf16[256,1792]{1,0:T(8,128)(2,1)S(1)}, bf16[256,1792]{1,0:T(8,128)(2,1)}, u32[]{:S(2)}) copy-start(bf16[256,1792]{1,0:T(8,128)(2,1)} %get-tuple-element.9) | copy-start | bytes 2752516
  173.4 1.5 copy-start.1
  173.4 2.4 %copy-start = (bf16[256,1792]{1,0:T(8,128)(2,1)S(1)}, bf16[256,1792]{1,0:T(8,128)(2,1)}, u32[]{:S(2)}) copy-start(bf16[256,1792]{1,0:T(8,128)(2,1)} %get-tuple-element.11) | copy-start | bytes 2752516
